TPU v7x, 32 devices: a whole 2x2x4 slice. The times are simulated.
32 devices in a mesh: ga: 8 (over y, x, core), band: 4 (over z).
Axes of the slice: x: 2, y: 2, z: 4, core: 2. Of those that a mesh axis runs over, the one named last changes fastest.
Arguments:
- psi: bfloat16 [2, 8, 96, 2048], P(None, 'band', None, 'ga'), may hold values from -6 to 6
- vloc: float32 [96, 9216], P('ga'), may hold values from 0.5 to 1.5
- dv: float32 [96, 9216], P('ga'), may hold values from -6 to 6
- beta: float32 [2, 128, 96, 2048], P(None, None, None, 'ga'), may hold values from -0.02734375 to 0.02734375
- dij: float32 [2, 4, 4], replicated, may hold values from -1 to 1.5, as said below
- atom_type: int32 [32], replicated, may hold values from 0 to 1
- stick_xy: int32 [2048], replicated, may hold values from 0 to 9215, as said below
- band_shift: float32 [8], P('band'), may hold values from 0.3 to 3
Outputs:
- response: float32 [2, 8, 96, 2048], P(None, 'band', None, 'ga')
- density: float32 [96, 9216], P('ga', 'band')
Inputs may be any that keep to these rules, and one draw needn't show every extreme that they name: `stick_xy`: 2048 distinct columns, each with both frequencies f(y) and f(x) in -(32) to 31. `dij`: each of the 2 matrices is symmetric positive definite with diagonal at least 0.5.
All inputs are finite; a program needn't handle non-finite values.
Results may differ from a plain program's by a relative error of at most 0.0003.
Values may be sent and summed in bfloat16 or wider, within the bound.
A program may use at most 128 MiB of HBM per device.

v0:
```python
import math

import jax
import jax.numpy as jnp
import ml_dtypes
import numpy as np
from jax import lax
from jax.experimental import pallas as pl
from jax.experimental.pallas import tpu as pltpu
from jax.sharding import PartitionSpec as P

LANES = 128
PER = 4
f32, bf16 = jnp.float32, jnp.bfloat16
VMEM = pl.BlockSpec(memory_space=pltpu.VMEM)


def frequency(index, grid):
    return (index + grid // 2) % grid - grid // 2


def phase(rows, cols, grid, sign):
    angle = 2.0 * math.pi * ((rows[:, None] * cols[None, :]) % grid) / grid
    return np.exp(1j * sign * angle) / math.sqrt(grid)


def parts_of(table):
    return np.stack(
        [np.stack([table.real, -table.imag], 1), np.stack([table.imag, table.real], 1)]
    )


def halves_of(table):
    table = table.astype(np.float32)
    hi = table.astype(ml_dtypes.bfloat16)
    lo = (table - hi.astype(np.float32)).astype(ml_dtypes.bfloat16)
    return hi, lo


class Plan:
    def __init__(self, bands, grid, own, planes, shards, sticks):
        self.bands, self.grid, self.own, self.planes = bands, grid, own, planes
        self.shards, self.sticks = shards, sticks
        self.side = 2 * (grid // 3)
        self.q = 2 * planes
        self.rows = -(-bands * self.q // 16) * 16
        self.images = bands * planes
        self.groups = self.side // PER
        self.fold = LANES // self.side
        self.tiles = PER // self.fold
        self.wide = PER * self.side
        side, fold, tiles, groups = self.side, self.fold, self.tiles, self.groups
        cells = np.arange(grid)
        freqs = np.arange(side) - grid // 3
        z = parts_of(phase(cells, cells, grid, 1.0))
        z = z.reshape(2, shards, planes, 2 * grid).transpose(1, 0, 2, 3)
        self.z_inv = np.stack(halves_of(z.reshape(shards * self.q, 2 * grid)))
        z = parts_of(phase(cells, cells, grid, -1.0))
        z = z.reshape(2, grid, 2, shards, planes).transpose(0, 1, 3, 2, 4)
        self.z_fwd = np.stack(halves_of(z.reshape(2 * grid, shards * self.q)))
        y = parts_of(phase(cells, freqs, grid, 1.0))
        y = y.reshape(2, grid, 2, groups, tiles, fold).transpose(0, 5, 1, 2, 4, 3)
        hi, lo = halves_of(y.reshape(2 * fold * grid, 2 * tiles * groups))
        self.y_inv = np.concatenate([hi, hi, lo], axis=1)
        x = parts_of(phase(freqs, cells, grid, 1.0).T).transpose(2, 3, 0, 1)
        x = np.repeat(x[:, None], fold, axis=1)
        x = np.pad(x, ((0, 0),) * 4 + ((0, LANES - grid),))
        self.x_inv = np.stack(halves_of(x.reshape(2 * LANES, 2 * LANES)))
        x = parts_of(phase(cells, freqs, grid, -1.0).T).transpose(2, 3, 0, 1)
        x = np.repeat(x[:, :, :, None], fold, axis=3)
        x = np.pad(x, ((0, 0), (0, LANES - grid)) + ((0, 0),) * 3)
        self.x_fwd = np.stack(halves_of(x.reshape(2 * LANES, 2 * LANES)))
        y = parts_of(phase(freqs, cells, grid, -1.0))
        y = y.reshape(2, groups, tiles, fold, 2 * grid).transpose(0, 3, 2, 1, 4)
        self.y_fwd = np.stack(halves_of(y.reshape(2 * side, 2 * grid)))


def dot(a, b):
    return jnp.dot(a, b, preferred_element_type=f32)


def dot_t(a, b):
    return lax.dot_general(a, b, (((1,), (1,)), ((), ())), preferred_element_type=f32)


def split(x):
    hi = x.astype(bf16)
    return hi, (x - hi.astype(f32)).astype(bf16)


def split3(x):
    hi = x.astype(bf16)
    rest = x - hi.astype(f32)
    mid = rest.astype(bf16)
    return hi, mid, (rest - mid.astype(f32)).astype(bf16)


def aligned(at, size):
    return pl.ds(pl.multiple_of(at * size, math.gcd(size, LANES)), size)


def spec_of(shape, dtype=f32):
    return jax.ShapeDtypeStruct(shape, dtype)


def lines_to_rows(p, held, oh, mask, left, sq):
    def spread(src, carry):
        at = aligned(src, p.own)
        hi, lo = split(held[src])
        for g in range(p.groups):
            keep = mask[g, :, at]
            for r in range(0, p.rows, 16):
                to = pl.ds(g * p.rows + r, 16)
                left[0, to, at] = hi[r : r + 16] * keep
                left[1, to, at] = lo[r : r + 16] * keep
        return carry

    lax.fori_loop(0, p.shards, spread, 0)
    made = dot(left[0], oh[...]) + dot(left[1], oh[...])
    for t in range(p.tiles):
        sq[t] = made[:, t * LANES : (t + 1) * LANES]


def rows_to_mixed(p, sq, y_inv, mixed):
    low = lax.broadcasted_iota(jnp.int32, (1, 2 * LANES), 1) % LANES < p.side

    def pair(at, carry):
        for b in range(p.bands):
            tiles = []
            for k in range(2):
                pieces = []
                for c in range(2):
                    n = b * p.q + c * p.planes + 2 * at + k
                    for t in range(p.tiles):
                        pieces.append(sq[t, pl.ds(n, p.groups, stride=p.rows), :])
                tiles.append(jnp.concatenate(pieces, axis=0))
            hi, lo = split(jnp.concatenate(tiles, axis=1))
            out = dot(y_inv[...], jnp.concatenate([hi, lo, hi], axis=0))
            both = [
                jnp.where(
                    low,
                    out[2 * c * p.grid : (2 * c + 1) * p.grid],
                    out[(2 * c + 1) * p.grid : (2 * c + 2) * p.grid],
                )
                for c in range(2)
            ]
            for k in range(2):
                lane = slice(k * LANES, (k + 1) * LANES)
                hi, lo = split(jnp.concatenate([both[0][:, lane], both[1][:, lane]], axis=1))
                to = aligned(b * p.planes + 2 * at + k, p.grid)
                mixed[0, to, :] = hi
                mixed[1, to, :] = lo
        return carry

    lax.fori_loop(0, p.planes // 2, pair, 0)


def mixed_to_field(p, mixed, x_inv, x_fwd, pot, field, spectrum, stat):
    some = math.gcd(p.planes, 4)
    size = some * p.grid

    for b in range(p.bands):

        def block(at, total, b=b):
            to = aligned(b * (p.planes // some) + at, size)
            hi, lo = mixed[0, to, :], mixed[1, to, :]
            one = dot(hi, x_inv[0]) + dot(lo, x_inv[0]) + dot(hi, x_inv[1])
            field[to, :] = one
            wide = pot[aligned(at, size), :]
            used = one * jnp.concatenate([wide, wide], axis=1)
            if spectrum is not None:
                hi, lo = split(used)
                spectrum[to, :] = dot(hi, x_fwd[0]) + dot(lo, x_fwd[0]) + dot(hi, x_fwd[1])
            if stat is not None:
                made = jnp.sum((used * one).reshape(size // 8, 8, 2 * LANES), axis=0)
                total = total + made[:, :LANES] + made[:, LANES:]
            return total

        total = lax.fori_loop(0, p.planes // some, block, jnp.zeros((8, LANES), f32))
        if stat is not None:
            stat[b] = total


def spectrum_to_lines(p, spectrum, y_fwd, oh_t, group_of, sq, left, lines):
    low = lax.broadcasted_iota(jnp.int32, (1, 2 * LANES), 1) % LANES < p.side
    half = p.side // p.fold

    def pair(at, carry):
        for b in range(p.bands):
            tiles = []
            for k in range(2):
                one = spectrum[aligned(b * p.planes + 2 * at + k, p.grid), :]
                tiles.append(jnp.concatenate([one[:, :LANES], one[:, LANES:]], axis=0))
            hi, lo = split(jnp.concatenate(tiles, axis=1))
            out = dot(y_fwd[0], hi) + dot(y_fwd[0], lo) + dot(y_fwd[1], hi)
            for c in range(2):
                from_ = c * p.side
                both = jnp.where(
                    low, out[from_ : from_ + half], out[from_ + half : from_ + 2 * half]
                )
                for k in range(2):
                    to = aligned(b * p.q + c * p.planes + 2 * at + k, p.groups)
                    for t in range(p.tiles):
                        sq[t, to, :] = both[
                            t * p.groups : (t + 1) * p.groups, k * LANES : (k + 1) * LANES
                        ]
        return carry

    lax.fori_loop(0, p.planes // 2, pair, 0)
    for g in range(p.groups):
        to = pl.ds(g * p.rows, p.rows)
        for t in range(p.tiles):
            hi, lo = split(sq[t, pl.ds(g, p.rows, stride=p.groups), :])
            left[0, to, t * LANES : (t + 1) * LANES] = hi
            left[1, to, t * LANES : (t + 1) * LANES] = lo

    def gather(dest, carry):
        at = aligned(dest, p.own)
        weights = oh_t[:, at]
        got = dot(left[0, :, : p.wide], weights) + dot(left[1, :, : p.wide], weights)
        kind = group_of[0:1, at]
        kept = got[: p.rows]
        for g in range(1, p.groups):
            kept = jnp.where(kind == g, got[g * p.rows : (g + 1) * p.rows], kept)
        lines[dest] = kept
        return carry

    lax.fori_loop(0, p.shards, gather, 0)


def planes_call(p, held, tables, pot, back, want_stat, name):
    oh, oh_t, mask, group_of = tables
    outs = [spec_of((p.images * p.grid, 2 * LANES))]
    if back:
        outs.append(spec_of((p.shards, p.rows, p.own)))
    if want_stat:
        outs.append(spec_of((p.bands, 8, LANES)))
    ins = [held, oh, mask, p.y_inv, p.x_inv, pot]
    if back:
        ins += [oh_t, group_of, p.x_fwd, p.y_fwd]
    many = p.groups * p.rows
    scratch = [
        pltpu.VMEM((2, many, p.sticks), bf16),
        pltpu.VMEM((p.tiles, many, LANES), f32),
        pltpu.VMEM((2, p.images * p.grid, 2 * LANES), bf16),
    ]
    if back:
        scratch.append(pltpu.VMEM((p.images * p.grid, 2 * LANES), f32))

    def kernel(*refs):
        refs = list(refs)
        held_r, oh_r, mask_r, y_inv_r, x_inv_r, pot_r = refs[:6]
        refs = refs[6:]
        if back:
            oh_t_r, group_r, x_fwd_r, y_fwd_r = refs[:4]
            refs = refs[4:]
        field_r = refs.pop(0)
        lines_r = refs.pop(0) if back else None
        stat_r = refs.pop(0) if want_stat else None
        left, sq, mixed = refs[:3]
        spectrum = refs[3] if back else None
        lines_to_rows(p, held_r, oh_r, mask_r, left, sq)
        rows_to_mixed(p, sq, y_inv_r, mixed)
        mixed_to_field(
            p, mixed, x_inv_r, x_fwd_r if back else None, pot_r, field_r, spectrum, stat_r
        )
        if back:
            spectrum_to_lines(p, spectrum, y_fwd_r, oh_t_r, group_r, sq, left, lines_r)

    return pl.pallas_call(
        kernel,
        out_shape=outs,
        in_specs=[VMEM] * len(ins),
        out_specs=[VMEM] * len(outs),
        scratch_shapes=scratch,
        name=name,
    )(*ins)


def greet(axis, count):
    me = lax.axis_index(axis)
    barrier = pltpu.get_barrier_semaphore()
    for hop in range(1, count):
        peer = lax.rem(me + hop, count)
        pl.semaphore_signal(
            barrier, inc=1, device_id={axis: peer}, device_id_type=pl.DeviceIdType.MESH
        )


def met(count):
    pl.semaphore_wait(pltpu.get_barrier_semaphore(), count - 1)


def pushes(axis, count, source, held, send_sem, recv_sem, scatter):
    me = lax.axis_index(axis)
    copies = []
    for hop in range(1, count):
        peer = lax.rem(me + hop, count)
        copies.append(
            pltpu.make_async_remote_copy(
                src_ref=source.at[peer] if scatter else source,
                dst_ref=held.at[me],
                send_sem=send_sem.at[hop - 1],
                recv_sem=recv_sem.at[hop - 1],
                device_id={axis: peer},
                device_id_type=pl.DeviceIdType.MESH,
            )
        )
    return copies


def sems(count):
    return [pltpu.SemaphoreType.DMA((count - 1,)), pltpu.SemaphoreType.DMA((count - 1,))]


def collect(p, held, out_r):
    me = lax.axis_index("ga")
    for hop in range(1, p.shards):
        src = lax.rem(me + hop, p.shards)
        out_r[src] = held[src]


def to_lines(p, values, z_inv, chunks, exact):
    for b in range(p.bands):
        value = values(b)
        if exact:
            hi = value
            out = dot(z_inv[0], hi) + dot(z_inv[1], hi)
        else:
            hi, lo = split(value)
            out = dot(z_inv[0], hi) + dot(z_inv[0], lo) + dot(z_inv[1], hi)
        for d in range(p.shards):
            chunks[d, b * p.q : (b + 1) * p.q, :] = out[d * p.q : (d + 1) * p.q]


def from_lines(p, held, joined, z_fwd, result):
    for b in range(p.bands):
        for src in range(p.shards):
            joined[src * p.q : (src + 1) * p.q, :] = held[src, b * p.q : (b + 1) * p.q, :]
        hi, lo = split(joined[...])
        out = dot(z_fwd[0], hi) + dot(z_fwd[0], lo) + dot(z_fwd[1], hi)
        result[0, b] = out[: p.grid]
        result[1, b] = out[p.grid :]


def first_call(p, psi):
    def kernel(psi_r, z_inv_r, out_r, chunks, held, send, recv):
        greet("ga", p.shards)
        me = lax.axis_index("ga")
        to_lines(
            p, lambda b: jnp.concatenate([psi_r[0, b], psi_r[1, b]], axis=0), z_inv_r, chunks, True
        )
        met(p.shards)
        copies = pushes("ga", p.shards, chunks, held, send, recv, True)
        for copy in copies:
            copy.start()
        out_r[me] = chunks[me]
        for copy in copies:
            copy.wait()
        collect(p, held, out_r)

    shape = (p.shards, p.rows, p.own)
    return pl.pallas_call(
        kernel,
        out_shape=spec_of(shape),
        in_specs=[VMEM] * 2,
        out_specs=VMEM,
        scratch_shapes=[pltpu.VMEM(shape, f32), pltpu.VMEM(shape, f32)] + sems(p.shards),
        compiler_params=pltpu.CompilerParams(collective_id=0, has_side_effects=True),
        name="first_exchange",
    )(psi, p.z_inv)


def rhs_call(p, lines, gathered, diag):
    many = gathered.shape[1]
    count = p.bands * many * 2
    tall = 16
    inv_norm = 1.0 / (2.0 * p.grid * p.sticks)

    def kernel(
        lines_r, psi_r, diag_r, z_fwd_r, z_inv_r, rhs_r, chunks_r, stat_r,
        held, joined, image, part, sums, send0, recv0, send1, recv1,
    ):
        greet("ga", p.shards)
        me = lax.axis_index("ga")
        met(p.shards)
        copies = pushes("ga", p.shards, lines_r, held, send0, recv0, True)
        for copy in copies:
            copy.start()
        held[me] = lines_r[me]
        for copy in copies:
            copy.wait()
        from_lines(p, held, joined, z_fwd_r, image)

        for n in range(p.bands):

            def overlap(t, acc, n=n):
                z = aligned(t, tall)
                acc = list(acc)
                for lane in range(0, p.own, LANES):
                    cut = pl.ds(lane, LANES)
                    i_re, i_im = image[0, n, z, cut], image[1, n, z, cut]
                    for m in range(many):
                        p_re = psi_r[0, m, z, cut].astype(f32)
                        p_im = psi_r[1, m, z, cut].astype(f32)
                        acc[2 * m] = acc[2 * m] + (p_re * i_re + p_im * i_im)
                        acc[2 * m + 1] = acc[2 * m + 1] + (p_re * i_im - p_im * i_re)
                return tuple(acc)

            zero = jnp.zeros((tall, LANES), f32)
            acc = lax.fori_loop(0, p.grid // tall, overlap, (zero,) * (2 * many))
            for m in range(2 * many):
                part[pl.ds(n * 2 * many + m, 1), :] = jnp.sum(acc[m], axis=0, keepdims=True)
        part[...] = jnp.broadcast_to(
            jnp.sum(part[...], axis=1, keepdims=True) * inv_norm, part.shape
        )
        copies = pushes("ga", p.shards, part, sums, send1, recv1, False)
        for copy in copies:
            copy.start()
        sums[me] = part[...]
        for copy in copies:
            copy.wait()
        inter = sums[0]
        for at in range(1, p.shards):
            inter = inter + sums[at]
        sums[0] = inter

        for n in range(p.bands):

            def right(t, acc, n=n):
                z = aligned(t, tall)
                norm, curve = acc
                for lane in range(0, p.own, LANES):
                    cut = pl.ds(lane, LANES)
                    re, im = -image[0, n, z, cut], -image[1, n, z, cut]
                    for m in range(many):
                        p_re = psi_r[0, m, z, cut].astype(f32)
                        p_im = psi_r[1, m, z, cut].astype(f32)
                        row = n * 2 * many + 2 * m
                        c_re = sums[0, row : row + 1, :]
                        c_im = sums[0, row + 1 : row + 2, :]
                        re = re + (c_re * p_re - c_im * p_im)
                        im = im + (c_im * p_re + c_re * p_im)
                    rhs_r[0, n, z, cut] = re
                    rhs_r[1, n, z, cut] = im
                    square = re * re + im * im
                    norm = norm + square
                    curve = curve + square * diag_r[n, z, cut]
                return norm, curve

            zero = jnp.zeros((tall, LANES), f32)
            norm, curve = lax.fori_loop(0, p.grid // tall, right, (zero, zero))
            stat_r[0, n] = norm[:8] + norm[8:]
            stat_r[1, n] = curve[:8] + curve[8:]
        to_lines(
            p, lambda b: jnp.concatenate([rhs_r[0, b], rhs_r[1, b]], axis=0), z_inv_r, chunks_r, False
        )

    shape = (p.shards, p.rows, p.own)
    mine = (2, p.bands, p.grid, p.own)
    return pl.pallas_call(
        kernel,
        out_shape=[spec_of(mine), spec_of(shape), spec_of((2, p.bands, 8, LANES))],
        in_specs=[VMEM] * 5,
        out_specs=[VMEM] * 3,
        scratch_shapes=[
            pltpu.VMEM(shape, f32),
            pltpu.VMEM((p.shards * p.q, p.own), f32),
            pltpu.VMEM(mine, f32),
            pltpu.VMEM((count, LANES), f32),
            pltpu.VMEM((p.shards, count, LANES), f32),
        ]
        + sems(p.shards)
        + sems(p.shards),
        compiler_params=pltpu.CompilerParams(collective_id=1, has_side_effects=True),
        name="right_side",
    )(lines, gathered, diag, p.z_fwd, p.z_inv)


def project_block(p, beta_r, vec_r, sums_r, base, group, unroll):
    _, some, grid, lanes = beta_r.shape
    for first in range(0, some, group):

        def body(t, sums, first=first):
            z = aligned(t, 8)
            sums = list(sums)
            for lane in range(0, lanes, LANES):
                cut = pl.ds(lane, LANES)
                v_re = [vec_r[0, b, z, cut] for b in range(p.bands)]
                v_im = [vec_r[1, b, z, cut] for b in range(p.bands)]
                for j in range(group):
                    b_re = beta_r[0, first + j, z, cut]
                    b_im = beta_r[1, first + j, z, cut]
                    for b in range(p.bands):
                        to = (j * p.bands + b) * 2
                        sums[to] = sums[to] + (b_re * v_re[b] + b_im * v_im[b])
                        sums[to + 1] = sums[to + 1] + (b_re * v_im[b] - b_im * v_re[b])
            return tuple(sums)

        zero = jnp.zeros((8, LANES), f32)
        sums = lax.fori_loop(0, grid // 8, body, (zero,) * (group * p.bands * 2), unroll=unroll)
        for j in range(group):
            for n in range(2 * p.bands):
                sums_r[n, pl.ds(base + first + j, 1), :] = jnp.sum(
                    sums[j * p.bands * 2 + n], axis=0, keepdims=True
                )


def lane_totals(p, sums_r, out_r):
    ones = jnp.ones((8, LANES), bf16)
    for n in range(2 * p.bands):
        hi, mid, lo = split3(sums_r[n])
        out_r[n : n + 1, :] = (dot_t(ones, hi) + dot_t(ones, mid) + dot_t(ones, lo))[0:1]


def project_call(p, beta, vec, chunks, number):
    parts, count, grid, own = beta.shape
    some = math.gcd(count, 32)
    steps = count // some

    def kernel(beta_r, vec_r, chunks_r, out_r, proj_r, sums, held, send, recv):
        step = pl.program_id(0)
        me = lax.axis_index("ga")
        copies = pushes("ga", p.shards, chunks_r, held, send, recv, True)

        @pl.when(step == 0)
        def _():
            greet("ga", p.shards)
            met(p.shards)
            for copy in copies:
                copy.start()
            out_r[me] = chunks_r[me]

        project_block(p, beta_r, vec_r, sums, step * some, 4, 3)

        @pl.when(step == steps - 1)
        def _():
            lane_totals(p, sums, proj_r)
            for copy in copies:
                copy.wait()
            collect(p, held, out_r)

    whole = lambda shape: pl.BlockSpec(shape, lambda i: (0,) * len(shape))
    return pl.pallas_call(
        kernel,
        grid=(steps,),
        out_shape=[spec_of(chunks.shape), spec_of((2 * p.bands, count))],
        in_specs=[
            pl.BlockSpec((parts, some, grid, own), lambda i: (0, i, 0, 0)),
            whole(vec.shape),
            VMEM,
        ],
        out_specs=[VMEM, whole((2 * p.bands, count))],
        scratch_shapes=[
            pltpu.VMEM((2 * p.bands, count, LANES), f32),
            pltpu.VMEM(chunks.shape, f32),
        ]
        + sems(p.shards),
        compiler_params=pltpu.CompilerParams(collective_id=number, has_side_effects=True),
        cost_estimate=pl.CostEstimate(
            flops=4 * beta.size * p.bands, bytes_accessed=4 * beta.size, transcendentals=0
        ),
        name=f"project_{number}",
    )(beta, vec, chunks)


def payload_of(p, proj_r, stat_r, field_stat_r, pay):
    pay[0 : 2 * p.bands, :] = proj_r[...]
    for b in range(p.bands):
        norm = jnp.sum(stat_r[0, b], axis=0, keepdims=True)
        curve = jnp.sum(stat_r[1, b] + field_stat_r[b], axis=0, keepdims=True)
        both = jnp.concatenate([norm, curve], axis=0)
        both = jnp.broadcast_to(jnp.sum(both, axis=1, keepdims=True), both.shape)
        pay[2 * p.bands + b : 2 * p.bands + b + 1, :] = both[0:1]
        pay[3 * p.bands + b : 3 * p.bands + b + 1, :] = both[1:2]


def couple_rows(p, total, pair_r, coef_r):
    ones = jnp.ones((LANES, LANES), bf16)
    energy = []
    for b in range(p.bands):
        made = 0.0
        for n in (2 * b, 2 * b + 1):
            row = total[n : n + 1]
            product = pair_r[...] * row
            hi, mid, lo = split3(product)
            coef = dot(hi, ones) + dot(mid, ones) + dot(lo, ones)
            if coef_r is not None:
                coef_r[n] = coef
            eye = (
                lax.broadcasted_iota(jnp.int32, coef.shape, 0)
                == lax.broadcasted_iota(jnp.int32, coef.shape, 1)
            )
            on_lanes = jnp.sum(jnp.where(eye, coef, 0.0), axis=0, keepdims=True)
            made = made + jnp.sum(on_lanes * row, axis=1, keepdims=True)
        energy.append(made)
    return energy


def spread_block(p, beta_r, coef_r, out_r, base, group):
    _, some, grid, lanes = beta_r.shape
    for lane in range(0, lanes, LANES):
        cut = pl.ds(lane, LANES)
        for first in range(0, some, group):
            coef = [
                [
                    jnp.broadcast_to(coef_r[n, pl.ds(base + first + j, 1), :], (8, LANES))
                    for n in range(2 * p.bands)
                ]
                for j in range(group)
            ]

            def body(t, carry, first=first, coef=coef, cut=cut):
                z = aligned(t, 8)
                re = [out_r[0, b, z, cut] for b in range(p.bands)]
                im = [out_r[1, b, z, cut] for b in range(p.bands)]
                for j in range(group):
                    b_re = beta_r[0, first + j, z, cut]
                    b_im = beta_r[1, first + j, z, cut]
                    for b in range(p.bands):
                        c_re, c_im = coef[j][2 * b], coef[j][2 * b + 1]
                        re[b] = re[b] + (b_re * c_re - b_im * c_im)
                        im[b] = im[b] + (b_re * c_im + b_im * c_re)
                for b in range(p.bands):
                    out_r[0, b, z, cut] = re[b]
                    out_r[1, b, z, cut] = im[b]
                return carry

            lax.fori_loop(0, grid // 8, body, 0, unroll=2)


def residual_call(p, beta, lines, rhs, diag, pair, proj, stat, field_stat, number):
    parts, count, grid, own = beta.shape
    some = math.gcd(count, 32)
    steps = count // some
    tall = 8
    payload = -(-4 * p.bands // 8) * 8

    def kernel(
        beta_r, lines_r, rhs_r, diag_r, pair_r, proj_r, stat_r, field_stat_r, z_fwd_r, z_inv_r,
        res_r, chunks_r, new_stat_r, step_r,
        held, joined, image, back, pay, sums, coef, send0, recv0, send1, recv1,
    ):
        step = pl.program_id(0)
        me = lax.axis_index("ga")
        copies = pushes("ga", p.shards, lines_r, held, send0, recv0, True)
        small = pushes("ga", p.shards, pay, sums, send1, recv1, False)

        @pl.when(step == 0)
        def _():
            greet("ga", p.shards)
            payload_of(p, proj_r, stat_r, field_stat_r, pay)
            met(p.shards)
            for copy in small:
                copy.start()
            for copy in copies:
                copy.start()
            sums[me] = pay[...]
            held[me] = lines_r[me]
            back[...] = jnp.zeros_like(back)
            for copy in small:
                copy.wait()
            total = sums[0]
            for at in range(1, p.shards):
                total = total + sums[at]
            energy = couple_rows(p, total, pair_r, coef)
            for b in range(p.bands):
                norm = total[2 * p.bands + b : 2 * p.bands + b + 1]
                curve = total[3 * p.bands + b : 3 * p.bands + b + 1] + energy[b]
                step_r[b : b + 1, :] = norm
                step_r[p.bands + b : p.bands + b + 1, :] = norm / curve

        spread_block(p, beta_r, coef, back, step * some, 8)

        @pl.when(step == steps - 1)
        def _():
            for copy in copies:
                copy.wait()
            from_lines(p, held, joined, z_fwd_r, image)
            for b in range(p.bands):
                alpha = step_r[p.bands + b : p.bands + b + 1, :]

                def fresh(t, acc, b=b, alpha=alpha):
                    z = aligned(t, tall)
                    norm, curve = acc
                    for lane in range(0, own, LANES):
                        cut = pl.ds(lane, LANES)
                        scale = diag_r[b, z, cut]
                        square = 0.0
                        for c in range(2):
                            r = rhs_r[c, b, z, cut]
                            made = scale * r + image[c, b, z, cut] + back[c, b, z, cut]
                            new = r - alpha * made
                            res_r[c, b, z, cut] = new
                            square = square + new * new
                        norm = norm + square
                        curve = curve + square * scale
                    return norm, curve

                zero = jnp.zeros((tall, LANES), f32)
                norm, curve = lax.fori_loop(0, grid // tall, fresh, (zero, zero))
                new_stat_r[0, b] = norm
                new_stat_r[1, b] = curve
            to_lines(
                p,
                lambda b: jnp.concatenate([res_r[0, b], res_r[1, b]], axis=0),
                z_inv_r,
                chunks_r,
                False,
            )

    shape = (p.shards, p.rows, p.own)
    mine = (2, p.bands, p.grid, p.own)
    return pl.pallas_call(
        kernel,
        grid=(steps,),
        out_shape=[
            spec_of(mine), spec_of(shape), spec_of((2, p.bands, 8, LANES)),
            spec_of((2 * p.bands, LANES)),
        ],
        in_specs=[pl.BlockSpec((parts, some, grid, own), lambda i: (0, i, 0, 0))] + [VMEM] * 9,
        out_specs=[VMEM] * 4,
        scratch_shapes=[
            pltpu.VMEM(shape, f32),
            pltpu.VMEM((p.shards * p.q, p.own), f32),
            pltpu.VMEM(mine, f32),
            pltpu.VMEM(mine, f32),
            pltpu.VMEM((payload, LANES), f32),
            pltpu.VMEM((p.shards, payload, LANES), f32),
            pltpu.VMEM((2 * p.bands, count, LANES), f32),
        ]
        + sems(p.shards)
        + sems(p.shards),
        compiler_params=pltpu.CompilerParams(collective_id=number, has_side_effects=True),
        cost_estimate=pl.CostEstimate(
            flops=4 * beta.size * p.bands, bytes_accessed=4 * beta.size, transcendentals=0
        ),
        name=f"residual_{number}",
    )(beta, lines, rhs, diag, pair, proj, stat, field_stat, p.z_fwd, p.z_inv)


def last_call(p, groups, rhs, res, pair, proj, stat, field_stat, step, fields, number):
    payload = -(-4 * p.bands // 8) * 8
    wide = p.grid // groups
    dense = p.planes % 4 == 0 and LANES - p.grid == p.grid // 3
    thick = p.planes * 3 // 4 if dense else p.planes
    rest = LANES - p.grid

    def kernel(
        rhs_r, res_r, pair_r, proj_r, stat_r, field_stat_r, step_r, psi_r, f0_r, f1_r,
        resp_r, dens_r,
        pay, sums, chunks, got, send0, recv0, send1, recv1,
    ):
        greet("ga", p.shards)
        greet("band", groups)
        payload_of(p, proj_r, stat_r, field_stat_r, pay)
        met(p.shards + groups - 1)
        me = lax.axis_index("ga")
        copies = pushes("ga", p.shards, pay, sums, send0, recv0, False)
        for copy in copies:
            copy.start()
        sums[me] = pay[...]
        for copy in copies:
            copy.wait()
        total = sums[0]
        for at in range(1, p.shards):
            total = total + sums[at]
        energy = couple_rows(p, total, pair_r, None)
        keep, alpha1 = [], []
        for b in range(p.bands):
            norm0 = step_r[b : b + 1, :]
            alpha0 = step_r[p.bands + b : p.bands + b + 1, :]
            norm1 = total[2 * p.bands + b : 2 * p.bands + b + 1]
            curve = total[3 * p.bands + b : 3 * p.bands + b + 1] + energy[b]
            ratio = norm1 / norm0
            alpha = norm1 / (curve - ratio * norm1 / alpha0)
            alpha1.append(alpha)
            keep.append(alpha0 + alpha * ratio)

        def plane(zp):
            made = 0.0
            for b in range(p.bands):
                at = aligned(b * p.planes + zp, p.grid)
                k2 = jnp.concatenate([keep[b], keep[b]], axis=1)
                a2 = jnp.concatenate([alpha1[b], alpha1[b]], axis=1)
                made = made + psi_r[at, :] * (k2 * f0_r[at, :] + a2 * f1_r[at, :])
            return 4.0 * (made[:, :LANES] + made[:, LANES:])

        lane = lax.broadcasted_iota(jnp.int32, (1, LANES), 1)

        def put(at, value):
            for g in range(groups):
                chunks[g, at] = value[g * wide : (g + 1) * wide]

        if dense:

            def four(i, carry):
                last = plane(4 * i + 3)
                for k in range(3):
                    moved = pltpu.roll(last, p.grid - k * rest, 1)
                    put(3 * i + k, jnp.where(lane < p.grid, plane(4 * i + k), moved))
                return carry

            lax.fori_loop(0, p.planes // 4, four, 0)
        else:

            def single(i, carry):
                put(i, plane(i))
                return carry

            lax.fori_loop(0, p.planes, single, 0)

        mine = lax.axis_index("band")
        copies = pushes("band", groups, chunks, got, send1, recv1, True)
        for copy in copies:
            copy.start()
        got[mine] = chunks[mine]
        for b in range(p.bands):

            def answer(t, carry, b=b):
                z = aligned(t, 8)
                for lane_at in range(0, p.own, LANES):
                    cut = pl.ds(lane_at, LANES)
                    for c in range(2):
                        resp_r[c, b, z, cut] = (
                            keep[b] * rhs_r[c, b, z, cut] + alpha1[b] * res_r[c, b, z, cut]
                        )
                return carry

            lax.fori_loop(0, p.grid // 8, answer, 0)
        for copy in copies:
            copy.wait()
        for at in range(thick):
            value = got[0, at]
            for g in range(1, groups):
                value = value + got[g, at]
            got[0, at] = value
        if dense:
            for i in range(p.planes // 4):
                last = jnp.zeros((wide, LANES), f32)
                for k in range(3):
                    value = got[0, 3 * i + k]
                    dens_r[4 * i + k] = value
                    moved = pltpu.roll(value, LANES - p.grid + k * rest, 1)
                    inside = (lane >= k * rest) & (lane < (k + 1) * rest)
                    last = jnp.where(inside, moved, last)
                dens_r[4 * i + 3] = last
        else:
            for at in range(p.planes):
                dens_r[at] = got[0, at]

    mine = (2, p.bands, p.grid, p.own)
    return pl.pallas_call(
        kernel,
        out_shape=[spec_of(mine), spec_of((p.planes, wide, LANES))],
        in_specs=[VMEM] * 10,
        out_specs=[VMEM] * 2,
        scratch_shapes=[
            pltpu.VMEM((payload, LANES), f32),
            pltpu.VMEM((p.shards, payload, LANES), f32),
            pltpu.VMEM((groups, thick, wide, LANES), f32),
            pltpu.VMEM((groups, thick, wide, LANES), f32),
        ]
        + sems(p.shards)
        + sems(groups),
        compiler_params=pltpu.CompilerParams(collective_id=number, has_side_effects=True),
        name="finish",
    )(rhs, res, pair, proj, stat, field_stat, step, *fields)


def per_device(groups, shards, psi, vloc, dv, beta, dij, atom_type, stick_xy, band_shift):
    _, bands, grid, own = psi.shape
    planes = vloc.shape[0]
    sticks = stick_xy.shape[0]
    p = Plan(bands, grid, own, planes, shards, sticks)
    radius = grid // 3
    per_atom = dij.shape[1]
    count = beta.shape[1]

    ky = frequency(stick_xy // grid, grid) + radius
    kx = frequency(stick_xy % grid, grid) + radius
    group = ky // PER
    slot = (ky % PER) * p.side + kx
    places = jnp.arange(p.wide, dtype=jnp.int32)
    oh = (slot[:, None] == places[None, :]).astype(bf16)
    oh_t = (slot[None, :] == places[:, None]).astype(bf16)
    kinds = jnp.arange(p.groups, dtype=jnp.int32)
    mask = jnp.broadcast_to(
        (group[None, None, :] == kinds[:, None, None]), (p.groups, 16, sticks)
    ).astype(bf16)
    group_of = jnp.broadcast_to(group[None, :], (8, sticks))
    tables = (oh, oh_t, mask, group_of)

    def widen(field):
        shaped = jnp.pad(field.reshape(planes, grid, grid), ((0, 0), (0, 0), (0, LANES - grid)))
        return shaped.reshape(planes * grid, LANES)

    start = lax.axis_index("ga") * own
    own_xy = lax.dynamic_slice_in_dim(stick_xy, start, own)
    freq_z = frequency(jnp.arange(grid, dtype=jnp.int32), grid)
    summed = (
        freq_z[:, None] ** 2
        + (frequency(own_xy // grid, grid) ** 2 + frequency(own_xy % grid, grid) ** 2)[None, :]
    )
    kinetic = summed.astype(f32) * (4.0 / (grid * grid))
    diag = kinetic[None] + band_shift[:, None, None]

    index = jnp.arange(count, dtype=jnp.int32)
    kind = jnp.arange(dij.shape[0], dtype=jnp.int32)
    chosen = (atom_type[:, None] == kind[None, :]).astype(f32)
    selected = jnp.sum(chosen[:, :, None, None] * dij[None], axis=1).reshape(count, per_atom)
    pair = jnp.where(
        (index // per_atom)[:, None] == (index // per_atom)[None, :],
        jnp.tile(selected, (1, count // per_atom)),
        0.0,
    )

    others = [
        lax.ppermute(psi, "band", [(src, (src + hop) % groups) for src in range(groups)])
        for hop in range(1, groups)
    ]
    gathered = jnp.concatenate([psi] + others, axis=1)

    held = first_call(p, psi)
    psi_real, lines = planes_call(p, held, tables, widen(dv), True, False, "planes_dv")
    rhs, chunks, stat0 = rhs_call(p, lines, gathered, diag)
    held, proj0 = project_call(p, beta, rhs, chunks, 2)
    pot = widen(vloc)
    field0, lines, plane0 = planes_call(p, held, tables, pot, True, True, "planes_rhs")
    res, chunks, stat1, step = residual_call(
        p, beta, lines, rhs, diag, pair, proj0, stat0, plane0, 3
    )
    held, proj1 = project_call(p, beta, res, chunks, 4)
    field1, plane1 = planes_call(p, held, tables, pot, False, True, "planes_res")
    response, density = last_call(
        p, groups, rhs, res, pair, proj1, stat1, plane1, step, (psi_real, field0, field1), 5
    )
    density = density[:, :, :grid].reshape(planes, grid * grid // groups)
    return (response, density)


def solution(mesh):
    placed = (
        P(None, "band", None, "ga"),
        P("ga", None),
        P("ga", None),
        P(None, None, None, "ga"),
        P(),
        P(),
        P(),
        P("band"),
    )
    groups, shards = mesh.shape["band"], mesh.shape["ga"]

    def body(*args):
        return per_device(groups, shards, *args)

    return jax.shard_map(
        body,
        mesh=mesh,
        in_specs=placed,
        out_specs=(P(None, "band", None, "ga"), P("ga", "band")),
        check_vma=False,
    )
```

profile of v0, /device:TPU:0, one launch (start us, length us, event | category | flops | bytes accessed | tf_op | source)
XLA Modules:
  0.0 166.0 jit_solution(15098153413356880597)
XLA Ops:
  0.6 4.1 %collective-permute-start.1 = (bf16[2,2,96,256]{3,2,1,0:T(8,128)(2,1)}, bf16[2,2,96,256]{3,2,1,0:T(8,128)(2,1)S(1)}, u32[]{:S(2)}, u32[]{:S(2)}) collective-permute-start(bf16[2,2,96,256]{3,2,1,0:T(8,128)(2,1)} %psi_r.1), channel_id=1, source_target_pairs={{0,2},{1,3},{2,0},{3,1},{4,6},{5,7},{6,4},{7,5},{8,10},{9,11},{10,... | collective-permute-start | bytes 589832 | tf_op jit(solution)/shard_map/ppermute | solution.py:919
  4.8 1.6 collective-permute-start
  6.4 2.2 %collective-permute-start.2 = (bf16[2,2,96,256]{3,2,1,0:T(8,128)(2,1)}, bf16[2,2,96,256]{3,2,1,0:T(8,128)(2,1)S(1)}, u32[]{:S(2)}, u32[]{:S(2)}) collective-permute-start(bf16[2,2,96,256]{3,2,1,0:T(8,128)(2,1)} %psi_r.1), channel_id=1, source_target_pairs={{0,3},{1,0},{2,1},{3,2},{4,7},{5,4},{6,5},{7,6},{8,11},{9,8},{10,9... | collective-permute-start | bytes 589832 | tf_op jit(solution)/shard_map/ppermute | solution.py:919
  8.6 0.7 add_select_fusion
  9.4 1.3 fusion.refs_1_
  10.7 1.2 fusion.1.refs_6_
  11.9 0.8 fusion.16
  12.7 0.7 compare_convert_fusion
  13.3 0.8 multiply_reduce_fusion
  14.1 0.1 copy.18
  14.2 0.1 tile.10
  14.3 0.1 copy.19
  14.5 9.6 %first_exchange.1.refs_0_ = f32[8,48,256]{2,1,0:T(8,128)} custom-call(bf16[2,2,96,256]{3,2,1,0:T(8,128)(2,1)} %psi_r.1, bf16[2,192,192]{2,1,0:T(8,128)(2,1)} %constant.128.clone.z_inv_r), custom_call_target="tpu_custom_call" | custom-call | tf_op jit(solution)/shard_map/first_exchange/pallas_call | solution.py:363
  24.1 0.2 reshape.142
  24.4 0.2 reshape.140
  24.6 0.9 pad.8
  25.4 0.9 pad.7
  26.4 0.8 broadcast_add_fusion.diag_r
  27.2 0.6 broadcast_in_dim.8.refs_7_
  27.8 1.2 broadcast_in_dim.7.refs_2_
  29.0 17.9 %planes_dv.1 = (f32[2304,256]{1,0:T(8,128)}, f32[8,48,256]{2,1,0:T(8,128)}) custom-call(f32[8,48,256]{2,1,0:T(8,128)} %first_exchange.1.refs_0_, bf16[2048,256]{1,0:T(8,128)(2,1)} %fusion.refs_1_, bf16[16,16,2048]{2,1,0:T(8,128)(2,1)} %broadcast_in_dim.7.refs_2_, bf16[384,192]{1,0:T(8,128)(2,1)} %constant.129.clone.refs_3_, ...), custom_call_target="tpu_custom_call" | custom-call | tf_op jit(solution)/shard_map/planes_dv/pallas_call | solution.py:270
  46.9 0.7 compare_select_fusion.pair_r
  47.6 1.0 pad_maximum_fusion.psi_r
  48.6 16.4 %right_side.1 = (f32[2,2,96,256]{3,2,1,0:T(8,128)}, f32[8,48,256]{2,1,0:T(8,128)}, f32[2,2,8,128]{3,2,1,0:T(8,128)}) custom-call(f32[8,48,256]{2,1,0:T(8,128)} %get-tuple-element.22.lines_r, bf16[2,8,96,256]{3,2,1,0:T(8,128)(2,1)} %pad_maximum_fusion.psi_r, f32[2,96,256]{2,1,0:T(8,128)} %broadcast_add_fusion.diag_r, ...), custom_call_target="tpu_custom_call" | custom-call | tf_op jit(solution)/shard_map/right_side/pallas_call | solution.py:461
  65.0 14.4 %project_2.1 = (f32[8,48,256]{2,1,0:T(8,128)}, f32[4,128]{1,0:T(4,128)}) custom-call(f32[2,128,96,256]{3,2,1,0:T(8,128)} %beta_r.5, f32[2,2,96,256]{3,2,1,0:T(8,128)} %get-tuple-element.23.vec_r.rhs_r, f32[8,48,256]{2,1,0:T(8,128)} %get-tuple-element.24.chunks_r), custom_call_target="tpu_custom_call" | custom-call | flops 50331648 | bytes 25165824 | tf_op jit(solution)/shard_map/project_2/pallas_call | solution.py:544
  79.4 17.8 %planes_rhs.1 = (f32[2304,256]{1,0:T(8,128)}, f32[8,48,256]{2,1,0:T(8,128)}, f32[2,8,128]{2,1,0:T(8,128)}) custom-call(f32[8,48,256]{2,1,0:T(8,128)} %get-tuple-element.25.refs_0_, bf16[2048,256]{1,0:T(8,128)(2,1)} %fusion.refs_1_, bf16[16,16,2048]{2,1,0:T(8,128)(2,1)} %broadcast_in_dim.7.refs_2_, bf16[384,192]{1,0:T(8,128)(2,1)} %constant.129.clone.refs_3_, ...), custom_call_target="tpu_custom_call" | custom-call | tf_op jit(solution)/shard_map/planes_rhs/pallas_call | solution.py:270
  97.3 20.5 %residual_3.1 = (f32[2,2,96,256]{3,2,1,0:T(8,128)}, f32[8,48,256]{2,1,0:T(8,128)}, f32[2,2,8,128]{3,2,1,0:T(8,128)}, f32[4,128]{1,0:T(4,128)}) custom-call(f32[2,128,96,256]{3,2,1,0:T(8,128)} %beta_r.5, f32[8,48,256]{2,1,0:T(8,128)} %get-tuple-element.26.lines_r, f32[2,2,96,256]{3,2,1,0:T(8,128)} %get-tuple-element.23.vec_r.rhs_r, ...), custom_call_target="tpu_custom_call" | custom-call | flops 50331648 | bytes 25165824 | tf_op jit(solution)/shard_map/residual_3/pallas_call | solution.py:714
  117.8 14.8 %project_4.1 = (f32[8,48,256]{2,1,0:T(8,128)}, f32[4,128]{1,0:T(4,128)}) custom-call(f32[2,128,96,256]{3,2,1,0:T(8,128)} %beta_r.5, f32[2,2,96,256]{3,2,1,0:T(8,128)} %get-tuple-element.30.vec_r.res_r, f32[8,48,256]{2,1,0:T(8,128)} %get-tuple-element.31.chunks_r), custom_call_target="tpu_custom_call" | custom-call | flops 50331648 | bytes 25165824 | tf_op jit(solution)/shard_map/project_4/pallas_call | solution.py:544
  132.6 10.0 %planes_res.1 = (f32[2304,256]{1,0:T(8,128)}, f32[2,8,128]{2,1,0:T(8,128)}) custom-call(f32[8,48,256]{2,1,0:T(8,128)} %get-tuple-element.34.refs_0_, bf16[2048,256]{1,0:T(8,128)(2,1)} %fusion.refs_1_, bf16[16,16,2048]{2,1,0:T(8,128)(2,1)} %broadcast_in_dim.7.refs_2_, bf16[384,192]{1,0:T(8,128)(2,1)} %constant.129.clone.refs_3_, ...), custom_call_target="tpu_custom_call" | custom-call | tf_op jit(solution)/shard_map/planes_res/pallas_call | solution.py:270
  142.6 20.0 %finish.1 = (f32[2,2,96,256]{3,2,1,0:T(8,128)}, f32[12,24,128]{2,1,0:T(8,128)}) custom-call(f32[2,2,96,256]{3,2,1,0:T(8,128)} %get-tuple-element.23.vec_r.rhs_r, f32[2,2,96,256]{3,2,1,0:T(8,128)} %get-tuple-element.30.vec_r.res_r, f32[128,128]{1,0:T(8,128)} %compare_select_fusion.pair_r, f32[4,128]{1,0:T(4,128)} %get-tuple-element.32.proj_r, ...), custom_call_target="tpu_custom_call" | custom-call | tf_op jit(solution)/shard_map/finish/pallas_call | solution.py:853
  162.6 1.7 %reshape.144 = f32[12,2304]{1,0:T(8,128)} reshape(f32[12,24,96]{2,1,0:T(8,128)} %bitcast.10) | data formatting | bytes 221184 | tf_op jit(solution)/shard_map/reshape | solution.py:938
  164.2 1.8 %copy.21 = f32[2,2,96,256]{3,2,1,0:T(8,128)} copy(f32[2,2,96,256]{3,2,1,0:T(8,128)} %get-tuple-element.46) | data formatting | bytes 786432
  (16 shorter events, 0.1 us)
Async XLA Ops:
  0.6 23.5 %copy-start.1 = (f32[12,9216]{1,0:T(8,128)S(1)}, f32[12,9216]{1,0:T(8,128)}, u32[]{:S(2)}) copy-start(f32[12,9216]{1,0:T(8,128)} %param.15) | copy-start | bytes 1327108
  0.6 23.7 %copy-start.2 = (f32[12,9216]{1,0:T(8,128)S(1)}, f32[12,9216]{1,0:T(8,128)}, u32[]{:S(2)}) copy-start(f32[12,9216]{1,0:T(8,128)} %param.16) | copy-start | bytes 1327108
  0.6 47.0 %collective-permute-start.1 = (bf16[2,2,96,256]{3,2,1,0:T(8,128)(2,1)}, bf16[2,2,96,256]{3,2,1,0:T(8,128)(2,1)S(1)}, u32[]{:S(2)}, u32[]{:S(2)}) collective-permute-start(bf16[2,2,96,256]{3,2,1,0:T(8,128)(2,1)} %psi_r.1), channel_id=1, source_target_pairs={{0,2},{1,3},{2,0},{3,1},{4,6},{5,7},{6,4},{7,5},{8,10},{9,11},{10,... | collective-permute-start | bytes 589832 | tf_op jit(solution)/shard_map/ppermute | solution.py:919
  4.8 42.8 %collective-permute-start = (bf16[2,2,96,256]{3,2,1,0:T(8,128)(2,1)}, bf16[2,2,96,256]{3,2,1,0:T(8,128)(2,1)S(1)}, u32[]{:S(2)}, u32[]{:S(2)}) collective-permute-start(bf16[2,2,96,256]{3,2,1,0:T(8,128)(2,1)} %psi_r.1), channel_id=1, source_target_pairs={{0,1},{1,2},{2,3},{3,0},{4,5},{5,6},{6,7},{7,4},{8,9},{9,10},{10,1... | collective-permute-start | bytes 589832 | tf_op jit(solution)/shard_map/ppermute | solution.py:919
  6.4 41.3 %collective-permute-start.2 = (bf16[2,2,96,256]{3,2,1,0:T(8,128)(2,1)}, bf16[2,2,96,256]{3,2,1,0:T(8,128)(2,1)S(1)}, u32[]{:S(2)}, u32[]{:S(2)}) collective-permute-start(bf16[2,2,96,256]{3,2,1,0:T(8,128)(2,1)} %psi_r.1), channel_id=1, source_target_pairs={{0,3},{1,0},{2,1},{3,2},{4,7},{5,4},{6,5},{7,6},{8,11},{9,8},{10,9... | collective-permute-start | bytes 589832 | tf_op jit(solution)/shard_map/ppermute | solution.py:919
  24.1 2.3 %copy-start.3 = (f32[2]{0:T(128)S(1)}, f32[2]{0:T(128)}, u32[]{:S(2)}) copy-start(f32[2]{0:T(128)} %param.21) | copy-start | bytes 28
  29.0 18.6 %copy-start = (bf16[2,2,96,256]{3,2,1,0:T(8,128)(2,1)S(1)}, bf16[2,2,96,256]{3,2,1,0:T(8,128)(2,1)}, u32[]{:S(2)}) copy-start(bf16[2,2,96,256]{3,2,1,0:T(8,128)(2,1)} %psi_r.1) | copy-start | bytes 589828
where the time goes:
time: 167 us; the launch traced here: 166 us
  Pallas kernels  141 us (84%)
  other arithmetic  8.06 us (5%)
  starting transfers between devices  7.95 us (5%)
  local copies, waits for them, and re-layouts  7.76 us (5%)
    pallas_call x3, Pallas kernels, planes_call(): pl.pallas_call(kernel, out_shape=outs, in_specs=[VMEM] * len(ins), out_sp...  45.7 us
    pallas_call x2, Pallas kernels, project_call(): pl.pallas_call(kernel, grid=(steps,), out_shape=[spec_of(chunks.shape), s...  29.2 us
    pallas_call x1, Pallas kernels, residual_call(): pl.pallas_call(kernel, grid=(steps,), out_shape=[spec_of(mine), spec_of(s...  20.5 us
    pallas_call x1, Pallas kernels, last_call(): pl.pallas_call(kernel, out_shape=[spec_of(mine), spec_of((p.planes, wide,...  20 us
    pallas_call x1, Pallas kernels, rhs_call(): pl.pallas_call(kernel, out_shape=[spec_of(mine), spec_of(shape), spec_of(...  16.4 us
    pallas_call x1, Pallas kernels, first_call(): pl.pallas_call(kernel, out_shape=spec_of(shape), in_specs=[VMEM] * 2, out...  9.64 us
    ppermute x3, starting transfers between devices, per_device(): lax.ppermute(psi, 'band', [(src, (src + hop) % groups) for src in range(g...  7.95 us
  transfers between devices with their start and end apart: 3, of which 0 were waited for; matrix products, arithmetic and copies ran while one was open for 7% of the time, Pallas kernels for 17%

commit v1 on v0

v1 whole, which is shorter than its diff:
```python
import math

import jax
import jax.numpy as jnp
import ml_dtypes
import numpy as np
from jax import lax
from jax.experimental import pallas as pl
from jax.experimental.pallas import tpu as pltpu
from jax.sharding import PartitionSpec as P

LANES = 128
PER = 4
f32, bf16 = jnp.float32, jnp.bfloat16
VMEM = pl.BlockSpec(memory_space=pltpu.VMEM)


def frequency(index, grid):
    return (index + grid // 2) % grid - grid // 2


def phase(rows, cols, grid, sign):
    angle = 2.0 * math.pi * ((rows[:, None] * cols[None, :]) % grid) / grid
    return np.exp(1j * sign * angle) / math.sqrt(grid)


def parts_of(table):
    return np.stack(
        [np.stack([table.real, -table.imag], 1), np.stack([table.imag, table.real], 1)]
    )


def halves_of(table):
    table = table.astype(np.float32)
    hi = table.astype(ml_dtypes.bfloat16)
    lo = (table - hi.astype(np.float32)).astype(ml_dtypes.bfloat16)
    return hi, lo


class Plan:
    def __init__(self, bands, grid, own, planes, shards, sticks, count):
        self.bands, self.grid, self.own, self.planes = bands, grid, own, planes
        self.shards, self.sticks, self.count = shards, sticks, count
        self.side = 2 * (grid // 3)
        self.q = 2 * planes
        self.rows = -(-bands * self.q // 16) * 16
        self.images = bands * planes
        self.groups = self.side // PER
        self.fold = LANES // self.side
        self.tiles = PER // self.fold
        self.wide = PER * self.side
        side, fold, tiles, groups = self.side, self.fold, self.tiles, self.groups
        cells = np.arange(grid)
        freqs = np.arange(side) - grid // 3
        z = parts_of(phase(cells, cells, grid, 1.0))
        z = z.reshape(2, shards, planes, 2 * grid).transpose(1, 0, 2, 3)
        self.z_inv = np.stack(halves_of(z.reshape(shards * self.q, 2 * grid)))
        z = parts_of(phase(cells, cells, grid, -1.0))
        z = z.reshape(2, grid, 2, shards, planes).transpose(0, 1, 3, 2, 4)
        self.z_fwd = np.stack(halves_of(z.reshape(2 * grid, shards * self.q)))
        y = parts_of(phase(cells, freqs, grid, 1.0))
        y = y.reshape(2, grid, 2, groups, tiles, fold).transpose(0, 5, 1, 2, 4, 3)
        hi, lo = halves_of(y.reshape(2 * fold * grid, 2 * tiles * groups))
        self.y_inv = np.concatenate([hi, hi, lo], axis=1)
        x = parts_of(phase(freqs, cells, grid, 1.0).T).transpose(2, 3, 0, 1)
        x = np.repeat(x[:, None], fold, axis=1)
        x = np.pad(x, ((0, 0),) * 4 + ((0, LANES - grid),))
        self.x_inv = np.stack(halves_of(x.reshape(2 * LANES, 2 * LANES)))
        x = parts_of(phase(cells, freqs, grid, -1.0).T).transpose(2, 3, 0, 1)
        x = np.repeat(x[:, :, :, None], fold, axis=3)
        x = np.pad(x, ((0, 0), (0, LANES - grid)) + ((0, 0),) * 3)
        self.x_fwd = np.stack(halves_of(x.reshape(2 * LANES, 2 * LANES)))
        y = parts_of(phase(freqs, cells, grid, -1.0))
        y = y.reshape(2, groups, tiles, fold, 2 * grid).transpose(0, 3, 2, 1, 4)
        self.y_fwd = np.stack(halves_of(y.reshape(2 * side, 2 * grid)))


def dot(a, b):
    return jnp.dot(a, b, preferred_element_type=f32)


def dot_t(a, b):
    return lax.dot_general(a, b, (((1,), (1,)), ((), ())), preferred_element_type=f32)


def split(x):
    hi = x.astype(bf16)
    return hi, (x - hi.astype(f32)).astype(bf16)


def split3(x):
    hi = x.astype(bf16)
    rest = x - hi.astype(f32)
    mid = rest.astype(bf16)
    return hi, mid, (rest - mid.astype(f32)).astype(bf16)


def aligned(at, size):
    return pl.ds(pl.multiple_of(at * size, math.gcd(size, LANES)), size)


def spec_of(shape, dtype=f32):
    return jax.ShapeDtypeStruct(shape, dtype)


def lines_to_rows(p, held, oh_t, mask, left, sq):
    def spread(src, carry):
        at = aligned(src, p.own)
        hi, lo = split(held[src])
        for g in range(p.groups):
            keep = mask[g, :, at]
            for r in range(0, p.rows, 16):
                to = pl.ds(g * p.rows + r, 16)
                left[0, to, at] = hi[r : r + 16] * keep
                left[1, to, at] = lo[r : r + 16] * keep
        return carry

    lax.fori_loop(0, p.shards, spread, 0)
    made = dot_t(left[0], oh_t[...]) + dot_t(left[1], oh_t[...])
    for t in range(p.tiles):
        sq[t] = made[:, t * LANES : (t + 1) * LANES]


def rows_to_mixed(p, sq, y_inv, mixed):
    low = lax.broadcasted_iota(jnp.int32, (1, 2 * LANES), 1) % LANES < p.side

    def pair(at, carry):
        for b in range(p.bands):
            tiles = []
            for k in range(2):
                pieces = []
                for c in range(2):
                    n = b * p.q + c * p.planes + 2 * at + k
                    for t in range(p.tiles):
                        pieces.append(sq[t, pl.ds(n, p.groups, stride=p.rows), :])
                tiles.append(jnp.concatenate(pieces, axis=0))
            hi, lo = split(jnp.concatenate(tiles, axis=1))
            out = dot(y_inv[...], jnp.concatenate([hi, lo, hi], axis=0))
            both = [
                jnp.where(
                    low,
                    out[2 * c * p.grid : (2 * c + 1) * p.grid],
                    out[(2 * c + 1) * p.grid : (2 * c + 2) * p.grid],
                )
                for c in range(2)
            ]
            for k in range(2):
                lane = slice(k * LANES, (k + 1) * LANES)
                hi, lo = split(jnp.concatenate([both[0][:, lane], both[1][:, lane]], axis=1))
                to = aligned(b * p.planes + 2 * at + k, p.grid)
                mixed[0, to, :] = hi
                mixed[1, to, :] = lo
        return carry

    lax.fori_loop(0, p.planes // 2, pair, 0)


def mixed_to_field(p, mixed, x_inv, x_fwd, pot, field, spectrum, stat):
    some = math.gcd(p.planes, 4)
    size = some * p.grid

    for b in range(p.bands):

        def block(at, total, b=b):
            to = aligned(b * (p.planes // some) + at, size)
            hi, lo = mixed[0, to, :], mixed[1, to, :]
            one = dot(hi, x_inv[0]) + dot(lo, x_inv[0]) + dot(hi, x_inv[1])
            field[to, :] = one
            wide = pot[aligned(at, size), :]
            used = one * jnp.concatenate([wide, wide], axis=1)
            if spectrum is not None:
                hi, lo = split(used)
                spectrum[to, :] = dot(hi, x_fwd[0]) + dot(lo, x_fwd[0]) + dot(hi, x_fwd[1])
            if stat is not None:
                made = jnp.sum((used * one).reshape(size // 8, 8, 2 * LANES), axis=0)
                total = total + made[:, :LANES] + made[:, LANES:]
            return total

        total = lax.fori_loop(0, p.planes // some, block, jnp.zeros((8, LANES), f32))
        if stat is not None:
            stat[b] = total


def spectrum_to_lines(p, spectrum, y_fwd, oh_t, rows_of, sq, left, lines, held, push):
    low = lax.broadcasted_iota(jnp.int32, (1, 2 * LANES), 1) % LANES < p.side
    half = p.side // p.fold

    def pair(at, carry):
        for b in range(p.bands):
            tiles = []
            for k in range(2):
                one = spectrum[aligned(b * p.planes + 2 * at + k, p.grid), :]
                tiles.append(jnp.concatenate([one[:, :LANES], one[:, LANES:]], axis=0))
            hi, lo = split(jnp.concatenate(tiles, axis=1))
            out = dot(y_fwd[0], hi) + dot(y_fwd[0], lo) + dot(y_fwd[1], hi)
            for c in range(2):
                from_ = c * p.side
                both = jnp.where(
                    low, out[from_ : from_ + half], out[from_ + half : from_ + 2 * half]
                )
                for k in range(2):
                    to = aligned(b * p.q + c * p.planes + 2 * at + k, p.groups)
                    for t in range(p.tiles):
                        sq[t, to, :] = both[
                            t * p.groups : (t + 1) * p.groups, k * LANES : (k + 1) * LANES
                        ]
        return carry

    lax.fori_loop(0, p.planes // 2, pair, 0)
    for g in range(p.groups):
        to = pl.ds(g * p.rows, p.rows)
        for t in range(p.tiles):
            hi, lo = split(sq[t, pl.ds(g, p.rows, stride=p.groups), :])
            left[0, to, t * LANES : (t + 1) * LANES] = hi
            left[1, to, t * LANES : (t + 1) * LANES] = lo

    def gather(dest):
        at = aligned(dest, p.own)
        weights = oh_t[:, at]
        got = dot(left[0, :, : p.wide], weights) + dot(left[1, :, : p.wide], weights)
        kind = rows_of[1:2, at]
        kept = got[: p.rows]
        for g in range(1, p.groups):
            kept = jnp.where(kind == g, got[g * p.rows : (g + 1) * p.rows], kept)
        return kept

    me = lax.axis_index("ga")

    def each(hop, carry):
        dest = lax.rem(me + hop, p.shards)
        lines[dest] = gather(dest)

        @pl.when(hop > 1)
        def _():
            push(hop - 1).start()

        return carry

    lax.fori_loop(1, p.shards, each, 0)
    held[me] = gather(me)
    push(p.shards - 1).start()


def greet(axis, count):
    me = lax.axis_index(axis)
    barrier = pltpu.get_barrier_semaphore()
    for hop in range(1, count):
        peer = lax.rem(me + hop, count)
        pl.semaphore_signal(
            barrier, inc=1, device_id={axis: peer}, device_id_type=pl.DeviceIdType.MESH
        )


def pusher(axis, count, source, held, sends, recvs, which, scatter):
    me = lax.axis_index(axis)

    def push(hop):
        peer = lax.rem(me + hop, count)
        return pltpu.make_async_remote_copy(
            src_ref=source.at[peer] if scatter else source,
            dst_ref=held.at[me],
            send_sem=sends.at[which, hop - 1],
            recv_sem=recvs.at[which, hop - 1],
            device_id={axis: peer},
            device_id_type=pl.DeviceIdType.MESH,
        )

    return push


def start_all(push, count):
    for hop in range(1, count):
        push(hop).start()


def wait_all(push, count):
    for hop in range(1, count):
        push(hop).wait()


def total_of(sums, count):
    total = sums[0]
    for at in range(1, count):
        total = total + sums[at]
    return total


def to_lines(p, value_of, z_inv, chunks, exact):
    for b in range(p.bands):
        value = value_of(b)
        if exact:
            out = dot(z_inv[0], value) + dot(z_inv[1], value)
        else:
            hi, lo = split(value)
            out = dot(z_inv[0], hi) + dot(z_inv[0], lo) + dot(z_inv[1], hi)
        for d in range(p.shards):
            chunks[d, b * p.q : (b + 1) * p.q, :] = out[d * p.q : (d + 1) * p.q]


def from_lines(p, held, joined, z_fwd, result):
    for b in range(p.bands):
        for src in range(p.shards):
            joined[src * p.q : (src + 1) * p.q, :] = held[src, b * p.q : (b + 1) * p.q, :]
        hi, lo = split(joined[...])
        out = dot(z_fwd[0], hi) + dot(z_fwd[0], lo) + dot(z_fwd[1], hi)
        result[0, b] = out[: p.grid]
        result[1, b] = out[p.grid :]


TALL = 16
JB = 4
SLOTS = 4


def fetch(p, beta_hbm, staged, sem, at):
    return pltpu.make_async_copy(
        beta_hbm.at[:, pl.ds(at * JB, JB)], staged.at[at % SLOTS], sem.at[at % SLOTS]
    )


def convert(p, beta_hbm, staged, sem, beta, first, last):
    chunks = p.count // JB
    for at in range(first, last):
        fetch(p, beta_hbm, staged, sem, at).wait()
        slot = at % SLOTS

        def one(j, carry, at=at, slot=slot):
            for c in range(2):
                hi, lo = split(staged[slot, c, j])
                beta[0, c, at * JB + j] = hi
                beta[1, c, at * JB + j] = lo
            return carry

        lax.fori_loop(0, JB, one, 0)
        if at + SLOTS < chunks:
            fetch(p, beta_hbm, staged, sem, at + SLOTS).start()


def stack_vector(p, vec, stacked):
    for zt in range(p.grid // TALL):
        for b in range(p.bands):
            for c in range(2):
                hi, lo = split(vec[c, b, zt * TALL : (zt + 1) * TALL, :])
                at = (2 * b + c) * 2 * TALL
                stacked[zt, at : at + TALL, :] = hi
                stacked[zt, at + TALL : at + 2 * TALL, :] = lo


def project(p, beta, stacked, acc, pay):
    cols = 4 * p.bands * TALL
    keep = (
        lax.broadcasted_iota(jnp.int32, (TALL, cols), 0)
        == lax.broadcasted_iota(jnp.int32, (TALL, cols), 1) % TALL
    )
    some = math.gcd(p.count, 32)
    acc[...] = jnp.zeros_like(acc)

    def tile(at, carry):
        zt = at // (p.count // some)
        first = lax.rem(at, p.count // some) * some
        z = aligned(zt, TALL)
        right = stacked[zt]
        for c in range(2):
            hi = beta[0, c, pl.ds(first, some), z, :].reshape(some * TALL, p.own)
            lo = beta[1, c, pl.ds(first, some), z, :].reshape(some * TALL, p.own)
            out = (dot_t(hi, right) + dot_t(lo, right)).reshape(some, TALL, cols)
            out = jnp.where(keep[None], out, 0.0)
            acc[c, pl.ds(first, some)] += out[:, :8] + out[:, 8:]
        return carry

    lax.fori_loop(0, (p.grid // TALL) * (p.count // some), tile, 0)
    row = lax.broadcasted_iota(jnp.int32, (8, cols), 0)
    kind = lax.broadcasted_iota(jnp.int32, (8, cols), 1) // (2 * TALL)
    same = (row // 2 == kind // 2) & (row < 2 * p.bands)
    plain = jnp.where(same & (row % 2 == kind % 2), 1.0, 0.0).astype(bf16)
    cross = jnp.where(
        same & (row % 2 != kind % 2), jnp.where(row % 2 == 0, 1.0, -1.0), 0.0
    ).astype(bf16)
    made = 0.0
    for c, pick in ((0, plain), (1, cross)):
        for piece in split3(jnp.sum(acc[c], axis=1)):
            made = made + dot_t(pick, piece)
    pay[0 : 2 * p.bands, :] = made[: 2 * p.bands]


def couple(p, total, pair):
    hi, mid, lo = split3(total)
    p_hi, p_mid, p_lo = split3(pair[...])
    made = (
        dot_t(hi, p_hi) + dot_t(hi, p_mid) + dot_t(mid, p_hi)
        + dot_t(hi, p_lo) + dot_t(mid, p_mid) + dot_t(lo, p_hi)
    )
    product = jnp.sum(made * total, axis=1, keepdims=True)
    energy = [product[2 * b : 2 * b + 1] + product[2 * b + 1 : 2 * b + 2] for b in range(p.bands)]
    return made, energy


def build_coefs(p, made, coefs):
    blocks = p.count // TALL
    wide = TALL * TALL
    lane = lax.broadcasted_iota(jnp.int32, (TALL, wide), 1) // TALL
    source = lax.broadcasted_iota(jnp.int32, (TALL, wide), 0)
    repeat = jnp.where(lane == source, 1.0, 0.0).astype(bf16)
    keep = (
        lax.broadcasted_iota(jnp.int32, (TALL, wide), 0)
        == lax.broadcasted_iota(jnp.int32, (TALL, wide), 1) % TALL
    )
    hi, mid, lo = split3(made)
    for jb in range(blocks):
        cut = slice(jb * TALL, (jb + 1) * TALL)
        full = dot(hi[:, cut], repeat) + dot(mid[:, cut], repeat) + dot(lo[:, cut], repeat)
        for b in range(p.bands):
            re, im = full[2 * b : 2 * b + 1], full[2 * b + 1 : 2 * b + 2]
            for part, rows in ((0, (re, im)), (1, (-im, re))):
                for c in range(2):
                    one, two = split(jnp.where(keep, rows[c], 0.0))
                    to = slice((2 * b + c) * TALL, (2 * b + c + 1) * TALL)
                    at = slice((2 * jb + part) * wide, (2 * jb + part + 1) * wide)
                    coefs[0, to, at] = one
                    coefs[1, to, at] = two


def back_project(p, beta, coefs, back):
    blocks = p.count // TALL
    wide = TALL * TALL
    many = 2 * p.bands * TALL

    def tile(zt, carry):
        z = aligned(zt, TALL)
        made = jnp.zeros((many, p.own), f32)
        for jb in range(blocks):
            for part in range(2):
                js = slice(jb * TALL, (jb + 1) * TALL)
                hi = beta[0, part, js, z, :].reshape(wide, p.own)
                lo = beta[1, part, js, z, :].reshape(wide, p.own)
                at = slice((2 * jb + part) * wide, (2 * jb + part + 1) * wide)
                c_hi, c_lo = coefs[0, :, at], coefs[1, :, at]
                made = made + dot(c_hi, hi) + dot(c_lo, hi) + dot(c_hi, lo)
        for b in range(p.bands):
            for c in range(2):
                at = (2 * b + c) * TALL
                back[c, b, z, :] = made[at : at + TALL]
        return carry

    lax.fori_loop(0, p.grid // TALL, tile, 0)


def intersect(p, groups, gath, image, part):
    many = groups * p.bands
    inv_norm = 1.0 / (2.0 * p.grid * p.sticks)
    for n in range(p.bands):

        def overlap(t, acc, n=n):
            z = aligned(t, TALL)
            acc = list(acc)
            for lane in range(0, p.own, LANES):
                cut = pl.ds(lane, LANES)
                i_re, i_im = image[0, n, z, cut], image[1, n, z, cut]
                for m in range(many):
                    p_re = gath[m // p.bands, 0, m % p.bands, z, cut].astype(f32)
                    p_im = gath[m // p.bands, 1, m % p.bands, z, cut].astype(f32)
                    re = p_re * i_re + p_im * i_im
                    im = p_re * i_im - p_im * i_re
                    acc[2 * m] = acc[2 * m] + (re[:8] + re[8:])
                    acc[2 * m + 1] = acc[2 * m + 1] + (im[:8] + im[8:])
            return tuple(acc)

        zero = jnp.zeros((8, LANES), f32)
        acc = lax.fori_loop(0, p.grid // TALL, overlap, (zero,) * (2 * many))
        for m in range(2 * many):
            part[pl.ds(n * 2 * many + m, 1), :] = jnp.sum(acc[m], axis=0, keepdims=True)
    part[...] = jnp.broadcast_to(
        jnp.sum(part[...], axis=1, keepdims=True) * inv_norm, part.shape
    )


def right_side(p, groups, gath, image, inter, diag, rhs):
    many = groups * p.bands
    stats = []
    for n in range(p.bands):

        def right(t, acc, n=n):
            z = aligned(t, TALL)
            norm, curve = acc
            for lane in range(0, p.own, LANES):
                cut = pl.ds(lane, LANES)
                re, im = -image[0, n, z, cut], -image[1, n, z, cut]
                for m in range(many):
                    p_re = gath[m // p.bands, 0, m % p.bands, z, cut].astype(f32)
                    p_im = gath[m // p.bands, 1, m % p.bands, z, cut].astype(f32)
                    row = n * 2 * many + 2 * m
                    c_re = inter[row : row + 1, :]
                    c_im = inter[row + 1 : row + 2, :]
                    re = re + (c_re * p_re - c_im * p_im)
                    im = im + (c_im * p_re + c_re * p_im)
                rhs[0, n, z, cut] = re
                rhs[1, n, z, cut] = im
                square = re * re + im * im
                norm = norm + square
                curve = curve + square * diag[n, z, cut]
            return norm, curve

        zero = jnp.zeros((TALL, LANES), f32)
        norm, curve = lax.fori_loop(0, p.grid // TALL, right, (zero, zero))
        stats.append((norm, curve))
    return stats


def fresh(p, rhs, image, back, diag, alpha, res):
    stats = []
    for b in range(p.bands):

        def one(t, acc, b=b):
            z = aligned(t, 8)
            norm, curve = acc
            for lane in range(0, p.own, LANES):
                cut = pl.ds(lane, LANES)
                scale = diag[b, z, cut]
                square = 0.0
                for c in range(2):
                    r = rhs[c, b, z, cut]
                    made = scale * r + image[c, b, z, cut] + back[c, b, z, cut]
                    new = r - alpha[b] * made
                    res[c, b, z, cut] = new
                    square = square + new * new
                norm = norm + square
                curve = curve + square * scale
            return norm, curve

        zero = jnp.zeros((8, LANES), f32)
        stats.append(lax.fori_loop(0, p.grid // 8, one, (zero, zero)))
    return stats


def everywhere(x):
    x = jnp.sum(x, axis=0, keepdims=True)
    return jnp.broadcast_to(jnp.sum(x, axis=1, keepdims=True), x.shape)


def pay_stats(p, stats, pay):
    for b in range(p.bands):
        at = 2 * p.bands + b
        pay[at : at + 1, :] = everywhere(stats[b][0])
        at = 3 * p.bands + b
        pay[at : at + 1, :] = everywhere(stats[b][1])


def program(p, groups, psi, pot_dv, pot_v, beta_hbm_array, rows_of, shift, pair):
    payload = -(-4 * p.bands // 8) * 8
    few = -(-p.bands // 8) * 8
    many = groups * p.bands
    inters = p.bands * many * 2
    wide_y = p.grid // groups
    dense = p.planes % 4 == 0 and LANES - p.grid == p.grid // 3
    thick = p.planes * 3 // 4 if dense else p.planes
    rest = LANES - p.grid
    chunk = (p.shards, p.rows, p.own)
    mine = (2, p.bands, p.grid, p.own)
    cells = p.images * p.grid
    many_rows = p.groups * p.rows
    n_chunks = p.count // JB

    def kernel(
        psi_r, pot_dv_r, pot_v_r, beta_hbm, rows_r, shift_r, pair_r,
        z_inv, z_fwd, y_inv, x_inv, x_fwd, y_fwd,
        resp_r, dens_r,
        oh_t, mask, left, sq, mixed, spectrum, field_p, field_0, field_1,
        chunk_a, chunk_b, held_a, held_b, held_c, held_d, held_e,
        gath, joined, image, rhs, res, diag, stat,
        part, sums_i, pay_a, sums_a, pay_b, sums_b, pay_c, sums_c, pay_d, sums_d,
        staged, beta, stacked, acc, coefs,
        dens_send, dens_got,
        beta_sem, sends, recvs, band_sends, band_recvs,
    ):
        me = lax.axis_index("ga")
        mine_band = lax.axis_index("band")

        def over(source, held, which, scatter):
            return pusher("ga", p.shards, source, held, sends, recvs, which, scatter)

        greet("ga", p.shards)
        greet("band", groups)
        for at in range(SLOTS):
            fetch(p, beta_hbm, staged, beta_sem, at).start()
        to_lines(
            p, lambda b: jnp.concatenate([psi_r[0, b], psi_r[1, b]], axis=0), z_inv, chunk_a, True
        )
        pl.semaphore_wait(pltpu.get_barrier_semaphore(), p.shards + groups - 2)
        push_a = over(chunk_a, held_a, 0, True)
        start_all(push_a, p.shards)
        push_psi = pusher("band", groups, psi_r, gath, band_sends, band_recvs, 0, False)
        start_all(push_psi, groups)
        held_a[me] = chunk_a[me]
        gath[mine_band] = psi_r[...]

        def table(at, carry):
            cut = aligned(at, LANES)
            slot = rows_r[0:1, cut]
            rows = lax.broadcasted_iota(jnp.int32, (p.wide, LANES), 0)
            oh_t[:, cut] = jnp.where(rows == slot, 1.0, 0.0).astype(bf16)
            kind = jnp.broadcast_to(rows_r[1:2, cut], (16, LANES))
            for g in range(p.groups):
                mask[g, :, cut] = jnp.where(kind == g, 1.0, 0.0).astype(bf16)
            return carry

        lax.fori_loop(0, p.sticks // LANES, table, 0)
        flat = rows_r[2:3, pl.ds(pl.multiple_of(me * p.own, LANES), p.own)]
        z = lax.broadcasted_iota(jnp.int32, (p.grid, p.own), 0)
        z = jnp.where(z < p.grid // 2, z, z - p.grid)
        kinetic = (z * z + flat).astype(f32) * (4.0 / (p.grid * p.grid))
        for b in range(p.bands):
            diag[b] = kinetic + shift_r[b]
        early = n_chunks // 2
        convert(p, beta_hbm, staged, beta_sem, beta, 0, early)
        wait_all(push_a, p.shards)

        lines_to_rows(p, held_a, oh_t, mask, left, sq)
        rows_to_mixed(p, sq, y_inv, mixed)
        mixed_to_field(p, mixed, x_inv, x_fwd, pot_dv_r, field_p, spectrum, None)
        push_b = over(chunk_b, held_b, 1, True)
        spectrum_to_lines(p, spectrum, y_fwd, oh_t, rows_r, sq, left, chunk_b, held_b, push_b)
        convert(p, beta_hbm, staged, beta_sem, beta, early, n_chunks)
        wait_all(push_psi, groups)
        wait_all(push_b, p.shards)

        from_lines(p, held_b, joined, z_fwd, image)
        intersect(p, groups, gath, image, part)
        push_i = over(part, sums_i, 2, False)
        start_all(push_i, p.shards)
        sums_i[me] = part[...]
        wait_all(push_i, p.shards)
        part[...] = total_of(sums_i, p.shards)
        stats = right_side(p, groups, gath, image, part, diag, rhs)
        to_lines(
            p, lambda b: jnp.concatenate([rhs[0, b], rhs[1, b]], axis=0), z_inv, chunk_a, False
        )
        stack_vector(p, rhs, stacked)
        push_c = over(chunk_a, held_c, 3, True)
        start_all(push_c, p.shards)
        held_c[me] = chunk_a[me]
        pay_stats(p, stats, pay_a)
        project(p, beta, stacked, acc, pay_a)
        push_pa = over(pay_a, sums_a, 4, False)
        start_all(push_pa, p.shards)
        sums_a[me] = pay_a[...]
        wait_all(push_c, p.shards)

        lines_to_rows(p, held_c, oh_t, mask, left, sq)
        rows_to_mixed(p, sq, y_inv, mixed)
        mixed_to_field(p, mixed, x_inv, x_fwd, pot_v_r, field_0, spectrum, stat)
        for b in range(p.bands):
            pay_b[b : b + 1, :] = everywhere(stat[b])
        push_pb = over(pay_b, sums_b, 5, False)
        start_all(push_pb, p.shards)
        sums_b[me] = pay_b[...]
        push_d = over(chunk_b, held_d, 6, True)
        spectrum_to_lines(p, spectrum, y_fwd, oh_t, rows_r, sq, left, chunk_b, held_d, push_d)
        wait_all(push_pa, p.shards)
        total = total_of(sums_a, p.shards)
        made, energy = couple(p, total, pair_r)
        build_coefs(p, made, coefs)
        back_project(p, beta, coefs, res)
        wait_all(push_pb, p.shards)
        planes = total_of(sums_b, p.shards)
        norm0, alpha0 = [], []
        for b in range(p.bands):
            norm0.append(total[2 * p.bands + b : 2 * p.bands + b + 1])
            curve = total[3 * p.bands + b : 3 * p.bands + b + 1] + planes[b : b + 1] + energy[b]
            alpha0.append(norm0[b] / curve)
        wait_all(push_d, p.shards)
        from_lines(p, held_d, joined, z_fwd, image)
        stats = fresh(p, rhs, image, res, diag, alpha0, res)
        to_lines(
            p, lambda b: jnp.concatenate([res[0, b], res[1, b]], axis=0), z_inv, chunk_a, False
        )
        stack_vector(p, res, stacked)
        push_e = over(chunk_a, held_e, 7, True)
        start_all(push_e, p.shards)
        held_e[me] = chunk_a[me]
        pay_stats(p, stats, pay_c)
        project(p, beta, stacked, acc, pay_c)
        push_pc = over(pay_c, sums_c, 8, False)
        start_all(push_pc, p.shards)
        sums_c[me] = pay_c[...]
        wait_all(push_e, p.shards)

        lines_to_rows(p, held_e, oh_t, mask, left, sq)
        rows_to_mixed(p, sq, y_inv, mixed)
        mixed_to_field(p, mixed, x_inv, None, pot_v_r, field_1, None, stat)
        for b in range(p.bands):
            pay_d[b : b + 1, :] = everywhere(stat[b])
        push_pd = over(pay_d, sums_d, 9, False)
        start_all(push_pd, p.shards)
        sums_d[me] = pay_d[...]
        wait_all(push_pc, p.shards)
        total = total_of(sums_c, p.shards)
        made, energy = couple(p, total, pair_r)
        wait_all(push_pd, p.shards)
        planes = total_of(sums_d, p.shards)
        keep, alpha1 = [], []
        for b in range(p.bands):
            norm1 = total[2 * p.bands + b : 2 * p.bands + b + 1]
            curve = total[3 * p.bands + b : 3 * p.bands + b + 1] + planes[b : b + 1] + energy[b]
            ratio = norm1 / norm0[b]
            alpha = norm1 / (curve - ratio * norm1 / alpha0[b])
            alpha1.append(alpha)
            keep.append(alpha0[b] + alpha * ratio)

        def plane(zp):
            made = 0.0
            for b in range(p.bands):
                at = aligned(b * p.planes + zp, p.grid)
                k2 = jnp.concatenate([keep[b], keep[b]], axis=1)
                a2 = jnp.concatenate([alpha1[b], alpha1[b]], axis=1)
                made = made + field_p[at, :] * (k2 * field_0[at, :] + a2 * field_1[at, :])
            return 4.0 * (made[:, :LANES] + made[:, LANES:])

        lane = lax.broadcasted_iota(jnp.int32, (1, LANES), 1)

        def put(at, value):
            for g in range(groups):
                dens_send[g, at] = value[g * wide_y : (g + 1) * wide_y]

        if dense:

            def four(i, carry):
                last = plane(4 * i + 3)
                for k in range(3):
                    moved = pltpu.roll(last, p.grid - k * rest, 1)
                    put(3 * i + k, jnp.where(lane < p.grid, plane(4 * i + k), moved))
                return carry

            lax.fori_loop(0, p.planes // 4, four, 0)
        else:

            def single(i, carry):
                put(i, plane(i))
                return carry

            lax.fori_loop(0, p.planes, single, 0)

        push_z = pusher("band", groups, dens_send, dens_got, band_sends, band_recvs, 1, True)
        start_all(push_z, groups)
        dens_got[mine_band] = dens_send[mine_band]
        for b in range(p.bands):

            def answer(t, carry, b=b):
                z = aligned(t, 8)
                for lane_at in range(0, p.own, LANES):
                    cut = pl.ds(lane_at, LANES)
                    for c in range(2):
                        resp_r[c, b, z, cut] = (
                            keep[b] * rhs[c, b, z, cut] + alpha1[b] * res[c, b, z, cut]
                        )
                return carry

            lax.fori_loop(0, p.grid // 8, answer, 0)
        wait_all(push_z, groups)

        def summed(at):
            value = dens_got[0, at]
            for g in range(1, groups):
                value = value + dens_got[g, at]
            return value

        if dense:
            for i in range(p.planes // 4):
                last = jnp.zeros((wide_y, LANES), f32)
                for k in range(3):
                    value = summed(3 * i + k)
                    dens_r[4 * i + k] = value
                    moved = pltpu.roll(value, LANES - p.grid + k * rest, 1)
                    inside = (lane >= k * rest) & (lane < (k + 1) * rest)
                    last = jnp.where(inside, moved, last)
                dens_r[4 * i + 3] = last
        else:
            for at in range(p.planes):
                dens_r[at] = summed(at)

    small = (p.shards, payload, LANES)
    tiny = (p.shards, few, LANES)
    scratch = [
        pltpu.VMEM((p.wide, p.sticks), bf16),
        pltpu.VMEM((p.groups, 16, p.sticks), bf16),
        pltpu.VMEM((2, many_rows, p.sticks), bf16),
        pltpu.VMEM((p.tiles, many_rows, LANES), f32),
        pltpu.VMEM((2, cells, 2 * LANES), bf16),
        pltpu.VMEM((cells, 2 * LANES), f32),
        pltpu.VMEM((cells, 2 * LANES), f32),
        pltpu.VMEM((cells, 2 * LANES), f32),
        pltpu.VMEM((cells, 2 * LANES), f32),
        pltpu.VMEM(chunk, f32),
        pltpu.VMEM(chunk, f32),
        pltpu.VMEM(chunk, f32),
        pltpu.VMEM(chunk, f32),
        pltpu.VMEM(chunk, f32),
        pltpu.VMEM(chunk, f32),
        pltpu.VMEM(chunk, f32),
        pltpu.VMEM((groups,) + mine, bf16),
        pltpu.VMEM((p.shards * p.q, p.own), f32),
        pltpu.VMEM(mine, f32),
        pltpu.VMEM(mine, f32),
        pltpu.VMEM(mine, f32),
        pltpu.VMEM((p.bands, p.grid, p.own), f32),
        pltpu.VMEM((p.bands, 8, LANES), f32),
        pltpu.VMEM((inters, LANES), f32),
        pltpu.VMEM((p.shards, inters, LANES), f32),
        pltpu.VMEM((payload, LANES), f32),
        pltpu.VMEM(small, f32),
        pltpu.VMEM((few, LANES), f32),
        pltpu.VMEM(tiny, f32),
        pltpu.VMEM((payload, LANES), f32),
        pltpu.VMEM(small, f32),
        pltpu.VMEM((few, LANES), f32),
        pltpu.VMEM(tiny, f32),
        pltpu.VMEM((SLOTS, 2, JB, p.grid, p.own), f32),
        pltpu.VMEM((2, 2, p.count, p.grid, p.own), bf16),
        pltpu.VMEM((p.grid // TALL, 4 * p.bands * TALL, p.own), bf16),
        pltpu.VMEM((2, p.count, 8, 4 * p.bands * TALL), f32),
        pltpu.VMEM((2, 2 * p.bands * TALL, 2 * p.count * TALL), bf16),
        pltpu.VMEM((groups, thick, wide_y, LANES), f32),
        pltpu.VMEM((groups, thick, wide_y, LANES), f32),
        pltpu.SemaphoreType.DMA((SLOTS,)),
        pltpu.SemaphoreType.DMA((10, p.shards - 1)),
        pltpu.SemaphoreType.DMA((10, p.shards - 1)),
        pltpu.SemaphoreType.DMA((2, groups - 1)),
        pltpu.SemaphoreType.DMA((2, groups - 1)),
    ]
    return pl.pallas_call(
        kernel,
        out_shape=[spec_of(mine), spec_of((p.planes, wide_y, LANES))],
        in_specs=[VMEM] * 3
        + [pl.BlockSpec(memory_space=pl.ANY), VMEM, pl.BlockSpec(memory_space=pltpu.SMEM)]
        + [VMEM] * 7,
        out_specs=[VMEM] * 2,
        scratch_shapes=scratch,
        compiler_params=pltpu.CompilerParams(
            collective_id=0, has_side_effects=True, vmem_limit_bytes=67_043_328
        ),
        name="response",
    )(
        psi, pot_dv, pot_v, beta_hbm_array, rows_of, shift, pair,
        p.z_inv, p.z_fwd, p.y_inv, p.x_inv, p.x_fwd, p.y_fwd,
    )


def per_device(groups, shards, psi, vloc, dv, beta, dij, atom_type, stick_xy, band_shift):
    _, bands, grid, own = psi.shape
    planes = vloc.shape[0]
    sticks = stick_xy.shape[0]
    count = beta.shape[1]
    p = Plan(bands, grid, own, planes, shards, sticks, count)
    radius = grid // 3
    per_atom = dij.shape[1]

    fy = frequency(stick_xy // grid, grid)
    fx = frequency(stick_xy % grid, grid)
    ky, kx = fy + radius, fx + radius
    rows_of = jnp.stack(
        [(ky % PER) * p.side + kx, ky // PER, fy * fy + fx * fx] + [jnp.zeros_like(fy)] * 5
    )

    def widen(field):
        shaped = jnp.pad(field.reshape(planes, grid, grid), ((0, 0), (0, 0), (0, LANES - grid)))
        return shaped.reshape(planes * grid, LANES)

    index = jnp.arange(count, dtype=jnp.int32)
    kind = jnp.arange(dij.shape[0], dtype=jnp.int32)
    chosen = (atom_type[:, None] == kind[None, :]).astype(f32)
    selected = jnp.sum(chosen[:, :, None, None] * dij[None], axis=1).reshape(count, per_atom)
    pair = jnp.where(
        (index // per_atom)[:, None] == (index // per_atom)[None, :],
        jnp.tile(selected, (1, count // per_atom)),
        0.0,
    )
    response, density = program(
        p, groups, psi, widen(dv), widen(vloc), beta, rows_of, band_shift, pair
    )
    density = density[:, :, :grid].reshape(planes, grid * grid // groups)
    return (response, density)


def solution(mesh):
    placed = (
        P(None, "band", None, "ga"),
        P("ga", None),
        P("ga", None),
        P(None, None, None, "ga"),
        P(),
        P(),
        P(),
        P("band"),
    )
    groups, shards = mesh.shape["band"], mesh.shape["ga"]

    def body(*args):
        return per_device(groups, shards, *args)

    return jax.shard_map(
        body,
        mesh=mesh,
        in_specs=placed,
        out_specs=(P(None, "band", None, "ga"), P("ga", "band")),
        check_vma=False,
    )
```

time: 167 us -> 120 us (0.72)
  Pallas kernels: 141 us -> 107 us
  starting transfers between devices: 7.95 us -> 0 us
  other arithmetic: 8.06 us -> 2.88 us
    pallas_call x9 -> x1, Pallas kernels: 141 us -> 107 us  [program(): pl.pallas_call(kernel, out_shape=[spec_of(mine), spec_of((p.planes, wide_...]
    ppermute x3 -> x0, starting transfers between devices: 7.95 us -> none  [per_device(): lax.ppermute(psi, 'band', [(src, (src + hop) % groups) for src in range(g...]
    convert_element_type x3 -> x0, other arithmetic: 2.55 us -> none  [the longest x1 1.31 us: per_device(): oh = (slot[:, None] == places[None, :]).astype(bf16)]
    reshape x2, local copies, waits for them, and re-layouts: 0.41 us -> 2.58 us  [widen(): field.reshape(planes, grid, grid)]
    broadcast_in_dim x2 -> x0, local copies, waits for them, and re-layouts: 1.82 us -> none  [the longest x1 1.19 us: per_device(): jnp.broadcast_to(group[None, None, :] == kinds[:, None, None], (p.groups,...]
  transfers between devices with their start and end apart: 3 -> 0, of which waited for: 0 -> 0; matrix products, arithmetic and copies ran while one was open for 7% -> 0% of each run, Pallas kernels for 17% -> 0%
where the time goes in v1:
time: 120 us
  Pallas kernels  107 us (89%)
  local copies, waits for them, and re-layouts  8.77 us (7%)
  other arithmetic  2.88 us (2%)
    pallas_call x1, Pallas kernels, program(): pl.pallas_call(kernel, out_shape=[spec_of(mine), spec_of((p.planes, wide_...  107 us
    reshape x2, local copies, waits for them, and re-layouts, widen(): field.reshape(planes, grid, grid)  2.58 us

profile of v1, /device:TPU:0, one launch (start us, length us, event | category | flops | bytes accessed | tf_op | source)
XLA Modules:
  0.0 119.7 jit_solution(12454983276253687418)
XLA Ops:
  0.6 0.7 multiply_add_fusion
  1.4 0.7 stack.19.rows_r
  2.1 1.3 %reshape.72 = f32[12,96,96]{2,1,0:T(8,128)S(1)} reshape(f32[12,9216]{1,0:T(8,128)} %param.16) | data formatting | bytes 884736 | tf_op jit(solution)/shard_map/reshape | solution.py:864
  3.4 0.9 pad.7
  4.3 1.3 %reshape.74 = f32[12,96,96]{2,1,0:T(8,128)S(1)} reshape(f32[12,9216]{1,0:T(8,128)} %param.15) | data formatting | bytes 884736 | tf_op jit(solution)/shard_map/reshape | solution.py:864
  5.6 0.9 pad.8
  6.4 0.7 compare_convert_fusion
  7.1 0.8 multiply_reduce_fusion
  7.8 0.1 copy.18
  8.0 0.1 tile.10
  8.1 0.1 copy.19
  8.2 0.7 compare_select_fusion.pair_r
  8.9 107.4 %response.1 = (f32[2,2,96,256]{3,2,1,0:T(8,128)}, f32[12,24,128]{2,1,0:T(8,128)}) custom-call(bf16[2,2,96,256]{3,2,1,0:T(8,128)(2,1)} %psi_r.1, f32[1152,128]{1,0:T(8,128)} %bitcast.9, f32[1152,128]{1,0:T(8,128)} %bitcast.10, f32[2,128,96,256]{3,2,1,0:T(8,128)} %beta_hbm.1, s32[8,2048]{1,0:T(8,128)} %stack.19.rows_r, f32[2]{0:T(128)} %shift_r.1, ...), custom_call_target="tpu_custom_call" | custom-call | tf_op jit(solution)/shard_map/response/pallas_call | solution.py:829
  116.3 1.7 %reshape.76 = f32[12,2304]{1,0:T(8,128)} reshape(f32[12,24,96]{2,1,0:T(8,128)} %bitcast.12) | data formatting | bytes 221184 | tf_op jit(solution)/shard_map/reshape | solution.py:879
  118.0 1.8 %copy.21 = f32[2,2,96,256]{3,2,1,0:T(8,128)} copy(f32[2,2,96,256]{3,2,1,0:T(8,128)} %get-tuple-element.11) | data formatting | bytes 786432
  (4 shorter events, 0.0 us)

commit v2 on v1

--- a/solution.py
+++ b/solution.py
@@ -49,6 +49,9 @@
         self.fold = LANES // self.side
         self.tiles = PER // self.fold
         self.wide = PER * self.side
+        self.row_step = self.rows + 8
+        self.group_step = self.groups + 8
+        self.pot_step = grid + 8
         side, fold, tiles, groups = self.side, self.fold, self.tiles, self.groups
         cells = np.arange(grid)
         freqs = np.arange(side) - grid // 3
@@ -117,8 +120,11 @@
 
     lax.fori_loop(0, p.shards, spread, 0)
     made = dot_t(left[0], oh_t[...]) + dot_t(left[1], oh_t[...])
-    for t in range(p.tiles):
-        sq[t] = made[:, t * LANES : (t + 1) * LANES]
+    for g in range(p.groups):
+        for t in range(p.tiles):
+            sq[t, pl.ds(g * p.row_step, p.rows), :] = made[
+                g * p.rows : (g + 1) * p.rows, t * LANES : (t + 1) * LANES
+            ]
 
 
 def rows_to_mixed(p, sq, y_inv, mixed):
@@ -132,7 +138,7 @@
                 for c in range(2):
                     n = b * p.q + c * p.planes + 2 * at + k
                     for t in range(p.tiles):
-                        pieces.append(sq[t, pl.ds(n, p.groups, stride=p.rows), :])
+                        pieces.append(sq[t, pl.ds(n, p.groups, stride=p.row_step), :])
                 tiles.append(jnp.concatenate(pieces, axis=0))
             hi, lo = split(jnp.concatenate(tiles, axis=1))
             out = dot(y_inv[...], jnp.concatenate([hi, lo, hi], axis=0))
@@ -166,7 +172,13 @@
             hi, lo = mixed[0, to, :], mixed[1, to, :]
             one = dot(hi, x_inv[0]) + dot(lo, x_inv[0]) + dot(hi, x_inv[1])
             field[to, :] = one
-            wide = pot[aligned(at, size), :]
+            wide = jnp.concatenate(
+                [
+                    pot[pl.ds(pl.multiple_of((at * some + k) * p.pot_step, 8), p.grid), :]
+                    for k in range(some)
+                ],
+                axis=0,
+            )
             used = one * jnp.concatenate([wide, wide], axis=1)
             if spectrum is not None:
                 hi, lo = split(used)
@@ -199,7 +211,8 @@
                     low, out[from_ : from_ + half], out[from_ + half : from_ + 2 * half]
                 )
                 for k in range(2):
-                    to = aligned(b * p.q + c * p.planes + 2 * at + k, p.groups)
+                    n = b * p.q + c * p.planes + 2 * at + k
+                    to = pl.ds(pl.multiple_of(n * p.group_step, 8), p.groups)
                     for t in range(p.tiles):
                         sq[t, to, :] = both[
                             t * p.groups : (t + 1) * p.groups, k * LANES : (k + 1) * LANES
@@ -210,7 +223,7 @@
     for g in range(p.groups):
         to = pl.ds(g * p.rows, p.rows)
         for t in range(p.tiles):
-            hi, lo = split(sq[t, pl.ds(g, p.rows, stride=p.groups), :])
+            hi, lo = split(sq[t, pl.ds(g, p.rows, stride=p.group_step), :])
             left[0, to, t * LANES : (t + 1) * LANES] = hi
             left[1, to, t * LANES : (t + 1) * LANES] = lo
 
@@ -218,7 +231,7 @@
         at = aligned(dest, p.own)
         weights = oh_t[:, at]
         got = dot(left[0, :, : p.wide], weights) + dot(left[1, :, : p.wide], weights)
-        kind = rows_of[1:2, at]
+        kind = rows_of[0:1, at]
         kept = got[: p.rows]
         for g in range(1, p.groups):
             kept = jnp.where(kind == g, got[g * p.rows : (g + 1) * p.rows], kept)
@@ -352,7 +365,7 @@
         lax.broadcasted_iota(jnp.int32, (TALL, cols), 0)
         == lax.broadcasted_iota(jnp.int32, (TALL, cols), 1) % TALL
     )
-    some = math.gcd(p.count, 32)
+    some = p.count
     acc[...] = jnp.zeros_like(acc)
 
     def tile(at, carry):
@@ -445,6 +458,89 @@
     lax.fori_loop(0, p.grid // TALL, tile, 0)
 
 
+TOP = 32767.0
+
+
+def tables(p, xy_r, shift_r, rows_s, oh_t, mask, diag):
+    radius = p.grid // 3
+
+    def centred(k):
+        return jnp.where(k < p.grid // 2, k, k - p.grid)
+
+    def table(at, carry):
+        cut = aligned(at, LANES)
+        xy = xy_r[pl.ds(at, 1), :]
+        y = ((xy.astype(f32) + 0.5) * (1.0 / p.grid)).astype(jnp.int32)
+        fy, fx = centred(y), centred(xy - y * p.grid)
+        group = (fy + radius) // PER
+        slot = (fy + radius - group * PER) * p.side + fx + radius
+        rows_s[0:1, cut] = group
+        rows_s[1:2, cut] = fy * fy + fx * fx
+        rows = lax.broadcasted_iota(jnp.int32, (p.wide, LANES), 0)
+        oh_t[:, cut] = jnp.where(rows == slot, 1.0, 0.0).astype(bf16)
+        kind = jnp.broadcast_to(group, (16, LANES))
+        for g in range(p.groups):
+            mask[g, :, cut] = jnp.where(kind == g, 1.0, 0.0).astype(bf16)
+        return carry
+
+    lax.fori_loop(0, p.sticks // LANES, table, 0)
+    me = lax.axis_index("ga")
+    flat = rows_s[1:2, pl.ds(pl.multiple_of(me * p.own, LANES), p.own)]
+    z = centred(lax.broadcasted_iota(jnp.int32, (p.grid, p.own), 0))
+    kinetic = (z * z + flat).astype(f32) * (4.0 / (p.grid * p.grid))
+    for b in range(p.bands):
+        diag[b] = kinetic + shift_r[b]
+
+
+def widen(p, raw, pot):
+    lane = lax.broadcasted_iota(jnp.int32, (1, LANES), 1)
+    for y in range(p.grid):
+        tile, off = divmod(y * p.grid, LANES)
+        value = raw[:, tile * LANES : (tile + 1) * LANES]
+        if off:
+            value = pltpu.roll(value, LANES - off, 1)
+        if off + p.grid > LANES:
+            more = raw[:, (tile + 1) * LANES : (tile + 2) * LANES]
+            value = jnp.where(lane < LANES - off, value, pltpu.roll(more, LANES - off, 1))
+        pot[pl.ds(y, p.planes, stride=p.pot_step), :] = value
+
+
+def narrow(p, wide_y, rows, out):
+    lane = lax.broadcasted_iota(jnp.int32, (1, LANES), 1)
+    made = None
+    for y in range(wide_y):
+        tile, off = divmod(y * p.grid, LANES)
+        value = rows[pl.ds(y, p.planes, stride=wide_y), :]
+        if off:
+            value = pltpu.roll(value, off, 1)
+        made = value if off == 0 else jnp.where(lane < off, made, value)
+        if off + p.grid >= LANES:
+            out[:, tile * LANES : (tile + 1) * LANES] = made
+            made = value
+    if wide_y * p.grid % LANES:
+        tile = wide_y * p.grid // LANES
+        out[:, tile * LANES :] = made[:, : wide_y * p.grid - tile * LANES]
+
+
+def build_pair(p, dij_r, type_r, pair):
+    kinds, per, _ = dij_r.shape
+    shape = (8, p.count)
+    row = lax.broadcasted_iota(jnp.int32, shape, 0)
+    col = lax.broadcasted_iota(jnp.int32, shape, 1)
+    for first in range(0, p.count, 8):
+        kind = jnp.zeros(shape, jnp.int32)
+        for a in range(first // per, (first + 8) // per):
+            kind = jnp.where((row + first) // per == a, type_r[a], kind)
+        value = jnp.zeros(shape, f32)
+        for t in range(kinds):
+            for i in range(per):
+                here = (kind == t) & (row % per == i)
+                for k in range(per):
+                    value = jnp.where(here & (col % per == k), dij_r[t, i, k], value)
+        value = jnp.where((row + first) // per == col // per, value, 0.0)
+        pair[pl.ds(first, 8), :] = value
+
+
 def intersect(p, groups, gath, image, part):
     many = groups * p.bands
     inv_norm = 1.0 / (2.0 * p.grid * p.sticks)
@@ -532,6 +628,34 @@
     return stats
 
 
+def answers(p, keep, alpha, rhs, res, out):
+    for b in range(p.bands):
+
+        def answer(t, carry, b=b):
+            z = aligned(t, 8)
+            for lane_at in range(0, p.own, LANES):
+                cut = pl.ds(lane_at, LANES)
+                for c in range(2):
+                    out[c, b, z, cut] = keep[b] * rhs[c, b, z, cut] + alpha[b] * res[c, b, z, cut]
+            return carry
+
+        lax.fori_loop(0, p.grid // 8, answer, 0)
+
+
+def settle(*arrays):
+    def kernel(*refs):
+        for source, target in zip(refs[: len(arrays)], refs[len(arrays) :]):
+            target[...] = source[...]
+
+    return pl.pallas_call(
+        kernel,
+        out_shape=[spec_of(x.shape) for x in arrays],
+        in_specs=[VMEM] * len(arrays),
+        out_specs=[VMEM] * len(arrays),
+        name="settle",
+    )(*arrays)
+
+
 def everywhere(x):
     x = jnp.sum(x, axis=0, keepdims=True)
     return jnp.broadcast_to(jnp.sum(x, axis=1, keepdims=True), x.shape)
@@ -545,7 +669,7 @@
         pay[at : at + 1, :] = everywhere(stats[b][1])
 
 
-def program(p, groups, psi, pot_dv, pot_v, beta_hbm_array, rows_of, shift, pair):
+def program(p, groups, psi, dv, vloc, beta_array, xy, shift, dij, atom_type):
     payload = -(-4 * p.bands // 8) * 8
     few = -(-p.bands // 8) * 8
     many = groups * p.bands
@@ -554,6 +678,8 @@
     dense = p.planes % 4 == 0 and LANES - p.grid == p.grid // 3
     thick = p.planes * 3 // 4 if dense else p.planes
     rest = LANES - p.grid
+    coded = dense and wide_y % 8 == 0
+    dense_rows = -(-thick * wide_y // 16) * 16
     chunk = (p.shards, p.rows, p.own)
     mine = (2, p.bands, p.grid, p.own)
     cells = p.images * p.grid
@@ -561,16 +687,16 @@
     n_chunks = p.count // JB
 
     def kernel(
-        psi_r, pot_dv_r, pot_v_r, beta_hbm, rows_r, shift_r, pair_r,
+        psi_r, dv_r, vloc_r, beta_hbm, xy_r, shift_r, dij_r, type_r,
         z_inv, z_fwd, y_inv, x_inv, x_fwd, y_fwd,
-        resp_r, dens_r,
-        oh_t, mask, left, sq, mixed, spectrum, field_p, field_0, field_1,
+        resp_o, dens_r,
+        rows_s, pot_dv, pot_v, pair, oh_t, mask, left, sq, mixed, spectrum, field_p, field_0, field_1,
         chunk_a, chunk_b, held_a, held_b, held_c, held_d, held_e,
         gath, joined, image, rhs, res, diag, stat,
         part, sums_i, pay_a, sums_a, pay_b, sums_b, pay_c, sums_c, pay_d, sums_d,
         staged, beta, stacked, acc, coefs,
-        dens_send, dens_got,
-        beta_sem, sends, recvs, band_sends, band_recvs,
+        dens_f, dens_q, dens_send, dens_got, scale_send, scale_got, dens_sum,
+        beta_sem, sends, recvs, band_sends, band_recvs, out_sem,
     ):
         me = lax.axis_index("ga")
         mine_band = lax.axis_index("band")
@@ -585,6 +711,8 @@
         to_lines(
             p, lambda b: jnp.concatenate([psi_r[0, b], psi_r[1, b]], axis=0), z_inv, chunk_a, True
         )
+        tables(p, xy_r, shift_r, rows_s, oh_t, mask, diag)
+        widen(p, dv_r, pot_dv)
         pl.semaphore_wait(pltpu.get_barrier_semaphore(), p.shards + groups - 2)
         push_a = over(chunk_a, held_a, 0, True)
         start_all(push_a, p.shards)
@@ -593,33 +721,18 @@
         held_a[me] = chunk_a[me]
         gath[mine_band] = psi_r[...]
 
-        def table(at, carry):
-            cut = aligned(at, LANES)
-            slot = rows_r[0:1, cut]
-            rows = lax.broadcasted_iota(jnp.int32, (p.wide, LANES), 0)
-            oh_t[:, cut] = jnp.where(rows == slot, 1.0, 0.0).astype(bf16)
-            kind = jnp.broadcast_to(rows_r[1:2, cut], (16, LANES))
-            for g in range(p.groups):
-                mask[g, :, cut] = jnp.where(kind == g, 1.0, 0.0).astype(bf16)
-            return carry
-
-        lax.fori_loop(0, p.sticks // LANES, table, 0)
-        flat = rows_r[2:3, pl.ds(pl.multiple_of(me * p.own, LANES), p.own)]
-        z = lax.broadcasted_iota(jnp.int32, (p.grid, p.own), 0)
-        z = jnp.where(z < p.grid // 2, z, z - p.grid)
-        kinetic = (z * z + flat).astype(f32) * (4.0 / (p.grid * p.grid))
-        for b in range(p.bands):
-            diag[b] = kinetic + shift_r[b]
-        early = n_chunks // 2
+        early, middle = n_chunks * 5 // 8, n_chunks * 13 // 16
         convert(p, beta_hbm, staged, beta_sem, beta, 0, early)
         wait_all(push_a, p.shards)
 
         lines_to_rows(p, held_a, oh_t, mask, left, sq)
         rows_to_mixed(p, sq, y_inv, mixed)
-        mixed_to_field(p, mixed, x_inv, x_fwd, pot_dv_r, field_p, spectrum, None)
+        mixed_to_field(p, mixed, x_inv, x_fwd, pot_dv, field_p, spectrum, None)
         push_b = over(chunk_b, held_b, 1, True)
-        spectrum_to_lines(p, spectrum, y_fwd, oh_t, rows_r, sq, left, chunk_b, held_b, push_b)
-        convert(p, beta_hbm, staged, beta_sem, beta, early, n_chunks)
+        spectrum_to_lines(p, spectrum, y_fwd, oh_t, rows_s, sq, left, chunk_b, held_b, push_b)
+        convert(p, beta_hbm, staged, beta_sem, beta, early, middle)
+        widen(p, vloc_r, pot_v)
+        build_pair(p, dij_r, type_r, pair)
         wait_all(push_psi, groups)
         wait_all(push_b, p.shards)
 
@@ -628,6 +741,7 @@
         push_i = over(part, sums_i, 2, False)
         start_all(push_i, p.shards)
         sums_i[me] = part[...]
+        convert(p, beta_hbm, staged, beta_sem, beta, middle, n_chunks)
         wait_all(push_i, p.shards)
         part[...] = total_of(sums_i, p.shards)
         stats = right_side(p, groups, gath, image, part, diag, rhs)
@@ -647,17 +761,17 @@
 
         lines_to_rows(p, held_c, oh_t, mask, left, sq)
         rows_to_mixed(p, sq, y_inv, mixed)
-        mixed_to_field(p, mixed, x_inv, x_fwd, pot_v_r, field_0, spectrum, stat)
+        mixed_to_field(p, mixed, x_inv, x_fwd, pot_v, field_0, spectrum, stat)
         for b in range(p.bands):
             pay_b[b : b + 1, :] = everywhere(stat[b])
         push_pb = over(pay_b, sums_b, 5, False)
         start_all(push_pb, p.shards)
         sums_b[me] = pay_b[...]
         push_d = over(chunk_b, held_d, 6, True)
-        spectrum_to_lines(p, spectrum, y_fwd, oh_t, rows_r, sq, left, chunk_b, held_d, push_d)
+        spectrum_to_lines(p, spectrum, y_fwd, oh_t, rows_s, sq, left, chunk_b, held_d, push_d)
         wait_all(push_pa, p.shards)
         total = total_of(sums_a, p.shards)
-        made, energy = couple(p, total, pair_r)
+        made, energy = couple(p, total, pair)
         build_coefs(p, made, coefs)
         back_project(p, beta, coefs, res)
         wait_all(push_pb, p.shards)
@@ -686,7 +800,7 @@
 
         lines_to_rows(p, held_e, oh_t, mask, left, sq)
         rows_to_mixed(p, sq, y_inv, mixed)
-        mixed_to_field(p, mixed, x_inv, None, pot_v_r, field_1, None, stat)
+        mixed_to_field(p, mixed, x_inv, None, pot_v, field_1, None, stat)
         for b in range(p.bands):
             pay_d[b : b + 1, :] = everywhere(stat[b])
         push_pd = over(pay_d, sums_d, 9, False)
@@ -694,7 +808,7 @@
         sums_d[me] = pay_d[...]
         wait_all(push_pc, p.shards)
         total = total_of(sums_c, p.shards)
-        made, energy = couple(p, total, pair_r)
+        made, energy = couple(p, total, pair)
         wait_all(push_pd, p.shards)
         planes = total_of(sums_d, p.shards)
         keep, alpha1 = [], []
@@ -716,74 +830,98 @@
             return 4.0 * (made[:, :LANES] + made[:, LANES:])
 
         lane = lax.broadcasted_iota(jnp.int32, (1, LANES), 1)
-
-        def put(at, value):
-            for g in range(groups):
-                dens_send[g, at] = value[g * wide_y : (g + 1) * wide_y]
-
         if dense:
 
             def four(i, carry):
                 last = plane(4 * i + 3)
                 for k in range(3):
                     moved = pltpu.roll(last, p.grid - k * rest, 1)
-                    put(3 * i + k, jnp.where(lane < p.grid, plane(4 * i + k), moved))
+                    dens_f[3 * i + k] = jnp.where(lane < p.grid, plane(4 * i + k), moved)
                 return carry
 
             lax.fori_loop(0, p.planes // 4, four, 0)
         else:
 
             def single(i, carry):
-                put(i, plane(i))
+                dens_f[i] = plane(i)
                 return carry
 
             lax.fori_loop(0, p.planes, single, 0)
+
+        if coded:
+            for g in range(groups):
+                for at in range(thick):
+                    value = dens_f[at, g * wide_y : (g + 1) * wide_y, :]
+                    top = jnp.max(jnp.abs(value), axis=0, keepdims=True)
+                    up = jnp.where(top > 1e-30, TOP / top, 0.0)
+                    dens_q[at * wide_y : (at + 1) * wide_y, :] = jnp.round(value * up)
+                    scale_send[g, at : at + 1, :] = top * (1.0 / TOP)
+                dens_send[g] = dens_q[...].astype(jnp.int16)
+        else:
+            for g in range(groups):
+                for at in range(thick):
+                    to = pl.ds(at * wide_y, wide_y)
+                    dens_send[g, to, :] = dens_f[at, g * wide_y : (g + 1) * wide_y, :]
 
         push_z = pusher("band", groups, dens_send, dens_got, band_sends, band_recvs, 1, True)
         start_all(push_z, groups)
-        dens_got[mine_band] = dens_send[mine_band]
-        for b in range(p.bands):
-
-            def answer(t, carry, b=b):
-                z = aligned(t, 8)
-                for lane_at in range(0, p.own, LANES):
-                    cut = pl.ds(lane_at, LANES)
-                    for c in range(2):
-                        resp_r[c, b, z, cut] = (
-                            keep[b] * rhs[c, b, z, cut] + alpha1[b] * res[c, b, z, cut]
-                        )
-                return carry
-
-            lax.fori_loop(0, p.grid // 8, answer, 0)
+        answers(p, keep, alpha1, rhs, res, image)
+        resp_copy = pltpu.make_async_copy(image, resp_o, out_sem.at[0])
+        if coded:
+            push_s = pusher("band", groups, scale_send, scale_got, band_sends, band_recvs, 2, True)
+            start_all(push_s, groups)
+        resp_copy.start()
+        if coded:
+            wait_all(push_s, groups)
         wait_all(push_z, groups)
-
-        def summed(at):
-            value = dens_got[0, at]
-            for g in range(1, groups):
-                value = value + dens_got[g, at]
-            return value
-
+        if coded:
+            base = pl.ds(pl.multiple_of(mine_band * wide_y, 8), wide_y)
+            total = [dens_f[at, base, :] for at in range(thick)]
+            for hop in range(1, groups):
+                src = lax.rem(mine_band + hop, groups)
+                dens_q[...] = dens_got[src].astype(f32)
+                for at in range(thick):
+                    total[at] = total[at] + (
+                        dens_q[at * wide_y : (at + 1) * wide_y, :] * scale_got[src, at : at + 1, :]
+                    )
+        else:
+            dens_got[mine_band] = dens_send[mine_band]
+            total = []
+            for at in range(thick):
+                to = pl.ds(at * wide_y, wide_y)
+                value = dens_got[0, to, :]
+                for g in range(1, groups):
+                    value = value + dens_got[g, to, :]
+                total.append(value)
         if dense:
             for i in range(p.planes // 4):
                 last = jnp.zeros((wide_y, LANES), f32)
                 for k in range(3):
-                    value = summed(3 * i + k)
-                    dens_r[4 * i + k] = value
+                    value = total[3 * i + k]
+                    dens_sum[pl.ds((4 * i + k) * wide_y, wide_y), :] = value
                     moved = pltpu.roll(value, LANES - p.grid + k * rest, 1)
                     inside = (lane >= k * rest) & (lane < (k + 1) * rest)
                     last = jnp.where(inside, moved, last)
-                dens_r[4 * i + 3] = last
+                dens_sum[pl.ds((4 * i + 3) * wide_y, wide_y), :] = last
         else:
             for at in range(p.planes):
-                dens_r[at] = summed(at)
+                dens_sum[pl.ds(at * wide_y, wide_y), :] = total[at]
+        narrow(p, wide_y, dens_sum, dens_r)
+        resp_copy.wait()
 
     small = (p.shards, payload, LANES)
     tiny = (p.shards, few, LANES)
     scratch = [
+        pltpu.VMEM((8, p.sticks), jnp.int32),
+        pltpu.VMEM((p.planes * p.pot_step, LANES), f32),
+        pltpu.VMEM((p.planes * p.pot_step, LANES), f32),
+        pltpu.VMEM((p.count, p.count), f32),
         pltpu.VMEM((p.wide, p.sticks), bf16),
         pltpu.VMEM((p.groups, 16, p.sticks), bf16),
         pltpu.VMEM((2, many_rows, p.sticks), bf16),
-        pltpu.VMEM((p.tiles, many_rows, LANES), f32),
+        pltpu.VMEM(
+            (p.tiles, max(p.groups * p.row_step, p.rows * p.group_step), LANES), f32
+        ),
         pltpu.VMEM((2, cells, 2 * LANES), bf16),
         pltpu.VMEM((cells, 2 * LANES), f32),
         pltpu.VMEM((cells, 2 * LANES), f32),
@@ -818,28 +956,36 @@
         pltpu.VMEM((p.grid // TALL, 4 * p.bands * TALL, p.own), bf16),
         pltpu.VMEM((2, p.count, 8, 4 * p.bands * TALL), f32),
         pltpu.VMEM((2, 2 * p.bands * TALL, 2 * p.count * TALL), bf16),
-        pltpu.VMEM((groups, thick, wide_y, LANES), f32),
-        pltpu.VMEM((groups, thick, wide_y, LANES), f32),
+        pltpu.VMEM((thick, p.grid, LANES), f32),
+        pltpu.VMEM((dense_rows, LANES), f32),
+        pltpu.VMEM((groups, dense_rows, LANES), jnp.int16 if coded else f32),
+        pltpu.VMEM((groups, dense_rows, LANES), jnp.int16 if coded else f32),
+        pltpu.VMEM((groups, -(-thick // 8) * 8, LANES), f32),
+        pltpu.VMEM((groups, -(-thick // 8) * 8, LANES), f32),
+        pltpu.VMEM((p.planes * wide_y, LANES), f32),
         pltpu.SemaphoreType.DMA((SLOTS,)),
         pltpu.SemaphoreType.DMA((10, p.shards - 1)),
         pltpu.SemaphoreType.DMA((10, p.shards - 1)),
-        pltpu.SemaphoreType.DMA((2, groups - 1)),
-        pltpu.SemaphoreType.DMA((2, groups - 1)),
+        pltpu.SemaphoreType.DMA((3, groups - 1)),
+        pltpu.SemaphoreType.DMA((3, groups - 1)),
+        pltpu.SemaphoreType.DMA((1,)),
     ]
+    hbm = pl.BlockSpec(memory_space=pl.ANY)
+    smem = pl.BlockSpec(memory_space=pltpu.SMEM)
     return pl.pallas_call(
         kernel,
-        out_shape=[spec_of(mine), spec_of((p.planes, wide_y, LANES))],
-        in_specs=[VMEM] * 3
-        + [pl.BlockSpec(memory_space=pl.ANY), VMEM, pl.BlockSpec(memory_space=pltpu.SMEM)]
-        + [VMEM] * 7,
-        out_specs=[VMEM] * 2,
+        out_shape=[
+            spec_of(mine), spec_of((p.planes, wide_y * p.grid)),
+        ],
+        in_specs=[VMEM] * 3 + [hbm, VMEM] + [smem] * 3 + [VMEM] * 6,
+        out_specs=[hbm, VMEM],
         scratch_shapes=scratch,
         compiler_params=pltpu.CompilerParams(
             collective_id=0, has_side_effects=True, vmem_limit_bytes=67_043_328
         ),
         name="response",
     )(
-        psi, pot_dv, pot_v, beta_hbm_array, rows_of, shift, pair,
+        psi, dv, vloc, beta_array, xy, shift, dij, atom_type,
         p.z_inv, p.z_fwd, p.y_inv, p.x_inv, p.x_fwd, p.y_fwd,
     )
 
@@ -850,34 +996,8 @@
     sticks = stick_xy.shape[0]
     count = beta.shape[1]
     p = Plan(bands, grid, own, planes, shards, sticks, count)
-    radius = grid // 3
-    per_atom = dij.shape[1]
-
-    fy = frequency(stick_xy // grid, grid)
-    fx = frequency(stick_xy % grid, grid)
-    ky, kx = fy + radius, fx + radius
-    rows_of = jnp.stack(
-        [(ky % PER) * p.side + kx, ky // PER, fy * fy + fx * fx] + [jnp.zeros_like(fy)] * 5
-    )
-
-    def widen(field):
-        shaped = jnp.pad(field.reshape(planes, grid, grid), ((0, 0), (0, 0), (0, LANES - grid)))
-        return shaped.reshape(planes * grid, LANES)
-
-    index = jnp.arange(count, dtype=jnp.int32)
-    kind = jnp.arange(dij.shape[0], dtype=jnp.int32)
-    chosen = (atom_type[:, None] == kind[None, :]).astype(f32)
-    selected = jnp.sum(chosen[:, :, None, None] * dij[None], axis=1).reshape(count, per_atom)
-    pair = jnp.where(
-        (index // per_atom)[:, None] == (index // per_atom)[None, :],
-        jnp.tile(selected, (1, count // per_atom)),
-        0.0,
-    )
-    response, density = program(
-        p, groups, psi, widen(dv), widen(vloc), beta, rows_of, band_shift, pair
-    )
-    density = density[:, :, :grid].reshape(planes, grid * grid // groups)
-    return (response, density)
+    xy = stick_xy.reshape(sticks // LANES, LANES)
+    return settle(*program(p, groups, psi, dv, vloc, beta, xy, band_shift, dij, atom_type))
 
 
 def solution(mesh):

time: 120 us -> 101 us (0.84)
  local copies, waits for them, and re-layouts: 8.77 us -> 0 us
  Pallas kernels: 107 us -> 100 us
  other arithmetic: 2.88 us -> 0 us
    pallas_call x1, Pallas kernels: 107 us -> 98.6 us  [program(): pl.pallas_call(kernel, out_shape=[spec_of(mine), spec_of((p.planes, wide_...]
    reshape x3 -> x0, local copies, waits for them, and re-layouts: 4.25 us -> none  [the longest x2 2.58 us: widen(): field.reshape(planes, grid, grid)]
    pallas_call x0 -> x1, Pallas kernels: none -> 1.85 us  [settle(): pl.pallas_call(kernel, out_shape=[spec_of(x.shape) for x in arrays], in_s...]
    unnamed x1 -> x0, local copies, waits for them, and re-layouts: 1.77 us -> none
    pad x2 -> x0, local copies, waits for them, and re-layouts: 1.73 us -> none  [widen(): jnp.pad(field.reshape(planes, grid, grid), ((0, 0), (0, 0), (0, LANES - g...]
where the time goes in v2:
time: 101 us
  Pallas kernels  100 us (99%)
    pallas_call x1, Pallas kernels, program(): pl.pallas_call(kernel, out_shape=[spec_of(mine), spec_of((p.planes, wide_...  98.6 us

profile of v2, /device:TPU:0, one launch (start us, length us, event | category | flops | bytes accessed | tf_op | source)
XLA Modules:
  0.0 101.1 jit_solution(10347214200031655319)
XLA Ops:
  0.6 98.6 %response.1 = (f32[2,2,96,256]{3,2,1,0:T(8,128)}, f32[12,2304]{1,0:T(8,128)}) custom-call(bf16[2,2,96,256]{3,2,1,0:T(8,128)(2,1)} %psi_r.1, f32[12,9216]{1,0:T(8,128)} %dv_r.1, f32[12,9216]{1,0:T(8,128)} %vloc_r.1, f32[2,128,96,256]{3,2,1,0:T(8,128)} %beta_hbm.1, s32[16,128]{1,0:T(8,128)} %bitcast.1, f32[2]{0:T(128)} %shift_r.1, f32[2,4,4]{2,1,0:T(4,128)} %dij_r.1, ...), custom_call_target="tpu_custom_call" | custom-call | tf_op jit(solution)/shard_map/response/pallas_call | solution.py:975
  99.2 1.8 %settle.1 = (f32[2,2,96,256]{3,2,1,0:T(8,128)}, f32[12,2304]{1,0:T(8,128)}) custom-call(f32[2,2,96,256]{3,2,1,0:T(8,128)} %get-tuple-element.4.refs_0_, f32[12,2304]{1,0:T(8,128)} %get-tuple-element.5.refs_1_), custom_call_target="tpu_custom_call" | custom-call | tf_op jit(solution)/shard_map/settle/pallas_call | solution.py:650

commit v3 on v2

--- a/solution.py
+++ b/solution.py
@@ -11,6 +11,7 @@
 
 LANES = 128
 PER = 4
+TALL = 16
 f32, bf16 = jnp.float32, jnp.bfloat16
 VMEM = pl.BlockSpec(memory_space=pltpu.VMEM)
 
@@ -41,6 +42,8 @@
     def __init__(self, bands, grid, own, planes, shards, sticks, count):
         self.bands, self.grid, self.own, self.planes = bands, grid, own, planes
         self.shards, self.sticks, self.count = shards, sticks, count
+        self.vector = count * 4 // 8 // TALL * TALL
+        self.matrix = count - self.vector
         self.side = 2 * (grid // 3)
         self.q = 2 * planes
         self.rows = -(-bands * self.q // 16) * 16
@@ -119,7 +122,9 @@
         return carry
 
     lax.fori_loop(0, p.shards, spread, 0)
-    made = dot_t(left[0], oh_t[...]) + dot_t(left[1], oh_t[...])
+    many = p.groups * p.rows
+    made = dot_t(left[...].reshape(2 * many, p.sticks), oh_t[...])
+    made = made[:many] + made[many:]
     for g in range(p.groups):
         for t in range(p.tiles):
             sq[t, pl.ds(g * p.row_step, p.rows), :] = made[
@@ -158,39 +163,48 @@
                 mixed[1, to, :] = lo
         return carry
 
-    lax.fori_loop(0, p.planes // 2, pair, 0)
+    lax.fori_loop(0, p.planes // 2, pair, 0, unroll=3)
 
 
 def mixed_to_field(p, mixed, x_inv, x_fwd, pot, field, spectrum, stat):
-    some = math.gcd(p.planes, 4)
-    size = some * p.grid
-
-    for b in range(p.bands):
-
-        def block(at, total, b=b):
-            to = aligned(b * (p.planes // some) + at, size)
+    size = p.planes * p.grid
+
+    def block(b, carry):
+        to = aligned(b, size)
+        hi, lo = mixed[0, to, :], mixed[1, to, :]
+        field[to, :] = dot(hi, x_inv[0]) + dot(lo, x_inv[0]) + dot(hi, x_inv[1])
+        return carry
+
+    lax.fori_loop(0, p.bands, block, 0)
+    if stat is not None:
+        stat[...] = jnp.zeros_like(stat)
+
+    def scaled(at, carry):
+        to = aligned(at, p.grid)
+        one = field[to, :]
+        rows = pl.ds(pl.multiple_of(lax.rem(at, p.planes) * p.pot_step, 8), p.grid)
+        wide = pot[rows, :]
+        used = one * jnp.concatenate([wide, wide], axis=1)
+        if spectrum is not None:
+            hi, lo = split(used)
+            mixed[0, to, :] = hi
+            mixed[1, to, :] = lo
+        if stat is not None:
+            made = jnp.sum((used * one).reshape(p.grid // 8, 8, 2 * LANES), axis=0)
+            b = at // p.planes
+            stat[b] = stat[b] + made[:, :LANES] + made[:, LANES:]
+        return carry
+
+    lax.fori_loop(0, p.images, scaled, 0)
+    if spectrum is not None:
+
+        def forth(b, carry):
+            to = aligned(b, size)
             hi, lo = mixed[0, to, :], mixed[1, to, :]
-            one = dot(hi, x_inv[0]) + dot(lo, x_inv[0]) + dot(hi, x_inv[1])
-            field[to, :] = one
-            wide = jnp.concatenate(
-                [
-                    pot[pl.ds(pl.multiple_of((at * some + k) * p.pot_step, 8), p.grid), :]
-                    for k in range(some)
-                ],
-                axis=0,
-            )
-            used = one * jnp.concatenate([wide, wide], axis=1)
-            if spectrum is not None:
-                hi, lo = split(used)
-                spectrum[to, :] = dot(hi, x_fwd[0]) + dot(lo, x_fwd[0]) + dot(hi, x_fwd[1])
-            if stat is not None:
-                made = jnp.sum((used * one).reshape(size // 8, 8, 2 * LANES), axis=0)
-                total = total + made[:, :LANES] + made[:, LANES:]
-            return total
-
-        total = lax.fori_loop(0, p.planes // some, block, jnp.zeros((8, LANES), f32))
-        if stat is not None:
-            stat[b] = total
+            spectrum[to, :] = dot(hi, x_fwd[0]) + dot(lo, x_fwd[0]) + dot(hi, x_fwd[1])
+            return carry
+
+        lax.fori_loop(0, p.bands, forth, 0)
 
 
 def spectrum_to_lines(p, spectrum, y_fwd, oh_t, rows_of, sq, left, lines, held, push):
@@ -204,7 +218,8 @@
                 one = spectrum[aligned(b * p.planes + 2 * at + k, p.grid), :]
                 tiles.append(jnp.concatenate([one[:, :LANES], one[:, LANES:]], axis=0))
             hi, lo = split(jnp.concatenate(tiles, axis=1))
-            out = dot(y_fwd[0], hi) + dot(y_fwd[0], lo) + dot(y_fwd[1], hi)
+            both = dot(y_fwd[...].reshape(4 * p.side, 2 * p.grid), hi)
+            out = both[: 2 * p.side] + both[2 * p.side :] + dot(y_fwd[0], lo)
             for c in range(2):
                 from_ = c * p.side
                 both = jnp.where(
@@ -219,7 +234,7 @@
                         ]
         return carry
 
-    lax.fori_loop(0, p.planes // 2, pair, 0)
+    lax.fori_loop(0, p.planes // 2, pair, 0, unroll=3)
     for g in range(p.groups):
         to = pl.ds(g * p.rows, p.rows)
         for t in range(p.tiles):
@@ -320,7 +335,6 @@
         result[1, b] = out[p.grid :]
 
 
-TALL = 16
 JB = 4
 SLOTS = 4
 
@@ -332,7 +346,7 @@
 
 
 def convert(p, beta_hbm, staged, sem, beta, first, last):
-    chunks = p.count // JB
+    chunks = p.matrix // JB
     for at in range(first, last):
         fetch(p, beta_hbm, staged, sem, at).wait()
         slot = at % SLOTS
@@ -359,41 +373,65 @@
                 stacked[zt, at + TALL : at + 2 * TALL, :] = lo
 
 
-def project(p, beta, stacked, acc, pay):
+def project(p, beta, beta_f, vec, stacked, acc, acc_f, pay):
     cols = 4 * p.bands * TALL
+    many = 2 * p.bands
     keep = (
         lax.broadcasted_iota(jnp.int32, (TALL, cols), 0)
         == lax.broadcasted_iota(jnp.int32, (TALL, cols), 1) % TALL
     )
-    some = p.count
     acc[...] = jnp.zeros_like(acc)
-
-    def tile(at, carry):
-        zt = at // (p.count // some)
-        first = lax.rem(at, p.count // some) * some
+    acc_f[...] = jnp.zeros_like(acc_f)
+
+    def tile(zt, carry):
         z = aligned(zt, TALL)
         right = stacked[zt]
         for c in range(2):
-            hi = beta[0, c, pl.ds(first, some), z, :].reshape(some * TALL, p.own)
-            lo = beta[1, c, pl.ds(first, some), z, :].reshape(some * TALL, p.own)
-            out = (dot_t(hi, right) + dot_t(lo, right)).reshape(some, TALL, cols)
+            hi = beta[0, c, :, z, :].reshape(p.matrix * TALL, p.own)
+            lo = beta[1, c, :, z, :].reshape(p.matrix * TALL, p.own)
+            out = (dot_t(hi, right) + dot_t(lo, right)).reshape(p.matrix, TALL, cols)
             out = jnp.where(keep[None], out, 0.0)
-            acc[c, pl.ds(first, some)] += out[:, :8] + out[:, 8:]
+            acc[c] += out[:, :8] + out[:, 8:]
+        for first in range(0, p.vector, 4):
+            sums = [[acc_f[n, first + j] for n in range(many)] for j in range(4)]
+            for part in range(TALL // 8):
+                rows = pl.ds(pl.multiple_of(zt * TALL + part * 8, 8), 8)
+                for lane in range(0, p.own, LANES):
+                    cut = pl.ds(lane, LANES)
+                    v_re = [vec[0, b, rows, cut] for b in range(p.bands)]
+                    v_im = [vec[1, b, rows, cut] for b in range(p.bands)]
+                    for j in range(4):
+                        b_re = beta_f[0, first + j, rows, cut]
+                        b_im = beta_f[1, first + j, rows, cut]
+                        for b in range(p.bands):
+                            sums[j][2 * b] = sums[j][2 * b] + (b_re * v_re[b] + b_im * v_im[b])
+                            sums[j][2 * b + 1] = sums[j][2 * b + 1] + (
+                                b_re * v_im[b] - b_im * v_re[b]
+                            )
+            for j in range(4):
+                for n in range(many):
+                    acc_f[n, first + j] = sums[j][n]
         return carry
 
-    lax.fori_loop(0, (p.grid // TALL) * (p.count // some), tile, 0)
+    lax.fori_loop(0, p.grid // TALL, tile, 0)
     row = lax.broadcasted_iota(jnp.int32, (8, cols), 0)
     kind = lax.broadcasted_iota(jnp.int32, (8, cols), 1) // (2 * TALL)
-    same = (row // 2 == kind // 2) & (row < 2 * p.bands)
+    same = (row // 2 == kind // 2) & (row < many)
     plain = jnp.where(same & (row % 2 == kind % 2), 1.0, 0.0).astype(bf16)
     cross = jnp.where(
         same & (row % 2 != kind % 2), jnp.where(row % 2 == 0, 1.0, -1.0), 0.0
     ).astype(bf16)
     made = 0.0
+    empty = jnp.zeros((p.vector, cols), f32)
     for c, pick in ((0, plain), (1, cross)):
-        for piece in split3(jnp.sum(acc[c], axis=1)):
+        for piece in split3(jnp.concatenate([jnp.sum(acc[c], axis=1), empty], axis=0)):
             made = made + dot_t(pick, piece)
-    pay[0 : 2 * p.bands, :] = made[: 2 * p.bands]
+    empty = jnp.zeros((p.matrix, LANES), f32)
+    for n in range(many):
+        mine = jnp.where(lax.broadcasted_iota(jnp.int32, (8, LANES), 0) == n, 1.0, 0.0)
+        for piece in split3(jnp.concatenate([empty, jnp.sum(acc_f[n], axis=1)], axis=0)):
+            made = made + dot_t(mine.astype(bf16), piece)
+    pay[0:many, :] = made[:many]
 
 
 def couple(p, total, pair):
@@ -408,8 +446,8 @@
     return made, energy
 
 
-def build_coefs(p, made, coefs):
-    blocks = p.count // TALL
+def build_coefs(p, made, coefs, coefs_f):
+    blocks = p.matrix // TALL
     wide = TALL * TALL
     lane = lax.broadcasted_iota(jnp.int32, (TALL, wide), 1) // TALL
     source = lax.broadcasted_iota(jnp.int32, (TALL, wide), 0)
@@ -418,6 +456,14 @@
         lax.broadcasted_iota(jnp.int32, (TALL, wide), 0)
         == lax.broadcasted_iota(jnp.int32, (TALL, wide), 1) % TALL
     )
+    ones = jnp.ones((p.count, LANES), bf16)
+    chosen = (
+        lax.broadcasted_iota(jnp.int32, (p.vector, p.count), 0) + p.matrix
+        == lax.broadcasted_iota(jnp.int32, (p.vector, p.count), 1)
+    )
+    for n in range(2 * p.bands):
+        hi, mid, lo = split3(jnp.where(chosen, made[n : n + 1], 0.0))
+        coefs_f[n] = dot(hi, ones) + dot(mid, ones) + dot(lo, ones)
     hi, mid, lo = split3(made)
     for jb in range(blocks):
         cut = slice(jb * TALL, (jb + 1) * TALL)
@@ -433,26 +479,44 @@
                     coefs[1, to, at] = two
 
 
-def back_project(p, beta, coefs, back):
-    blocks = p.count // TALL
+def back_project(p, beta, beta_f, coefs, coefs_f, back):
+    blocks = p.matrix // TALL
     wide = TALL * TALL
     many = 2 * p.bands * TALL
 
     def tile(zt, carry):
         z = aligned(zt, TALL)
         made = jnp.zeros((many, p.own), f32)
+        places = [
+            (part, pl.ds(pl.multiple_of(zt * TALL + part * 8, 8), 8), lane)
+            for part in range(TALL // 8)
+            for lane in range(0, p.own, LANES)
+        ]
+        sums = [[0.0] * (2 * p.bands) for _ in places]
         for jb in range(blocks):
             for part in range(2):
                 js = slice(jb * TALL, (jb + 1) * TALL)
                 hi = beta[0, part, js, z, :].reshape(wide, p.own)
                 lo = beta[1, part, js, z, :].reshape(wide, p.own)
                 at = slice((2 * jb + part) * wide, (2 * jb + part + 1) * wide)
-                c_hi, c_lo = coefs[0, :, at], coefs[1, :, at]
-                made = made + dot(c_hi, hi) + dot(c_lo, hi) + dot(c_hi, lo)
-        for b in range(p.bands):
-            for c in range(2):
-                at = (2 * b + c) * TALL
-                back[c, b, z, :] = made[at : at + TALL]
+                both = dot(coefs[:, :, at].reshape(2 * many, wide), hi)
+                made = made + both[:many] + both[many:] + dot(coefs[0, :, at], lo)
+            for j in range(p.vector * jb // blocks, p.vector * (jb + 1) // blocks):
+                rows_c = [coefs_f[n, j : j + 1, :] for n in range(2 * p.bands)]
+                for mine, (part, rows, lane) in zip(sums, places):
+                    b_re = beta_f[0, j, rows, pl.ds(lane, LANES)]
+                    b_im = beta_f[1, j, rows, pl.ds(lane, LANES)]
+                    for b in range(p.bands):
+                        c_re, c_im = rows_c[2 * b], rows_c[2 * b + 1]
+                        mine[2 * b] = mine[2 * b] + (b_re * c_re - b_im * c_im)
+                        mine[2 * b + 1] = mine[2 * b + 1] + (b_re * c_im + b_im * c_re)
+        for mine, (part, rows, lane) in zip(sums, places):
+            for b in range(p.bands):
+                for c in range(2):
+                    at = (2 * b + c) * TALL + part * 8
+                    back[c, b, rows, pl.ds(lane, LANES)] = (
+                        made[at : at + 8, lane : lane + LANES] + mine[2 * b + c]
+                    )
         return carry
 
     lax.fori_loop(0, p.grid // TALL, tile, 0)
@@ -541,7 +605,19 @@
         pair[pl.ds(first, 8), :] = value
 
 
-def intersect(p, groups, gath, image, part):
+def spread_rows(pay, part):
+    rows = part.shape[0]
+    here = lax.broadcasted_iota(jnp.int32, (rows, rows), 0) == lax.broadcasted_iota(
+        jnp.int32, (rows, rows), 1
+    )
+    ones = jnp.ones((rows, LANES), bf16)
+    made = 0.0
+    for piece in split3(jnp.where(here, pay[0:1], 0.0)):
+        made = made + dot(piece, ones)
+    part[...] = made
+
+
+def intersect(p, groups, gath, image, part, pay):
     many = groups * p.bands
     inv_norm = 1.0 / (2.0 * p.grid * p.sticks)
     for n in range(p.bands):
@@ -565,9 +641,11 @@
         acc = lax.fori_loop(0, p.grid // TALL, overlap, (zero,) * (2 * many))
         for m in range(2 * many):
             part[pl.ds(n * 2 * many + m, 1), :] = jnp.sum(acc[m], axis=0, keepdims=True)
-    part[...] = jnp.broadcast_to(
-        jnp.sum(part[...], axis=1, keepdims=True) * inv_norm, part.shape
-    )
+    ones = jnp.ones((8, LANES), bf16)
+    made = 0.0
+    for piece in split3(part[...]):
+        made = made + dot_t(ones, piece)
+    pay[...] = made * inv_norm
 
 
 def right_side(p, groups, gath, image, inter, diag, rhs):
@@ -684,19 +762,20 @@
     mine = (2, p.bands, p.grid, p.own)
     cells = p.images * p.grid
     many_rows = p.groups * p.rows
-    n_chunks = p.count // JB
+    n_chunks = p.matrix // JB
 
     def kernel(
-        psi_r, dv_r, vloc_r, beta_hbm, xy_r, shift_r, dij_r, type_r,
-        z_inv, z_fwd, y_inv, x_inv, x_fwd, y_fwd,
+        psi_h, dv_h, vloc_h, beta_hbm, xy_h, shift_r, dij_r, type_r,
+        z_inv_h, z_fwd_h, y_inv_h, x_inv_h, x_fwd_h, y_fwd_h,
         resp_o, dens_r,
         rows_s, pot_dv, pot_v, pair, oh_t, mask, left, sq, mixed, spectrum, field_p, field_0, field_1,
         chunk_a, chunk_b, held_a, held_b, held_c, held_d, held_e,
         gath, joined, image, rhs, res, diag, stat,
-        part, sums_i, pay_a, sums_a, pay_b, sums_b, pay_c, sums_c, pay_d, sums_d,
-        staged, beta, stacked, acc, coefs,
+        part, pay_i, sums_i, pay_a, sums_a, pay_b, sums_b, pay_c, sums_c, pay_d, sums_d,
+        staged, beta, beta_f, stacked, acc, acc_f, coefs, coefs_f,
         dens_f, dens_q, dens_send, dens_got, scale_send, scale_got, dens_sum,
         beta_sem, sends, recvs, band_sends, band_recvs, out_sem,
+        psi_r, dv_r, vloc_r, xy_r, z_inv, z_fwd, y_inv, x_inv, x_fwd, y_fwd, in_sem,
     ):
         me = lax.axis_index("ga")
         mine_band = lax.axis_index("band")
@@ -706,13 +785,25 @@
 
         greet("ga", p.shards)
         greet("band", groups)
+        loads = [
+            pltpu.make_async_copy(source, target, in_sem.at[i])
+            for i, (source, target) in enumerate(
+                (
+                    (psi_h, psi_r), (z_inv_h, z_inv), (xy_h, xy_r), (dv_h, dv_r),
+                    (y_inv_h, y_inv), (x_inv_h, x_inv), (x_fwd_h, x_fwd), (y_fwd_h, y_fwd),
+                    (z_fwd_h, z_fwd), (vloc_h, vloc_r),
+                )
+            )
+        ]
+        for load in loads:
+            load.start()
         for at in range(SLOTS):
             fetch(p, beta_hbm, staged, beta_sem, at).start()
+        loads[0].wait()
+        loads[1].wait()
         to_lines(
             p, lambda b: jnp.concatenate([psi_r[0, b], psi_r[1, b]], axis=0), z_inv, chunk_a, True
         )
-        tables(p, xy_r, shift_r, rows_s, oh_t, mask, diag)
-        widen(p, dv_r, pot_dv)
         pl.semaphore_wait(pltpu.get_barrier_semaphore(), p.shards + groups - 2)
         push_a = over(chunk_a, held_a, 0, True)
         start_all(push_a, p.shards)
@@ -720,9 +811,17 @@
         start_all(push_psi, groups)
         held_a[me] = chunk_a[me]
         gath[mine_band] = psi_r[...]
-
-        early, middle = n_chunks * 5 // 8, n_chunks * 13 // 16
+        for load in loads[2:]:
+            load.wait()
+        tables(p, xy_r, shift_r, rows_s, oh_t, mask, diag)
+        widen(p, dv_r, pot_dv)
+
+        early, middle = n_chunks * 7 // 8, n_chunks
         convert(p, beta_hbm, staged, beta_sem, beta, 0, early)
+        rest_copy = pltpu.make_async_copy(
+            beta_hbm.at[:, pl.ds(p.matrix, p.vector)], beta_f, out_sem.at[1]
+        )
+        rest_copy.start()
         wait_all(push_a, p.shards)
 
         lines_to_rows(p, held_a, oh_t, mask, left, sq)
@@ -737,13 +836,14 @@
         wait_all(push_b, p.shards)
 
         from_lines(p, held_b, joined, z_fwd, image)
-        intersect(p, groups, gath, image, part)
-        push_i = over(part, sums_i, 2, False)
+        intersect(p, groups, gath, image, part, pay_i)
+        push_i = over(pay_i, sums_i, 2, False)
         start_all(push_i, p.shards)
-        sums_i[me] = part[...]
+        sums_i[me] = pay_i[...]
         convert(p, beta_hbm, staged, beta_sem, beta, middle, n_chunks)
+        rest_copy.wait()
         wait_all(push_i, p.shards)
-        part[...] = total_of(sums_i, p.shards)
+        spread_rows(total_of(sums_i, p.shards), part)
         stats = right_side(p, groups, gath, image, part, diag, rhs)
         to_lines(
             p, lambda b: jnp.concatenate([rhs[0, b], rhs[1, b]], axis=0), z_inv, chunk_a, False
@@ -753,7 +853,7 @@
         start_all(push_c, p.shards)
         held_c[me] = chunk_a[me]
         pay_stats(p, stats, pay_a)
-        project(p, beta, stacked, acc, pay_a)
+        project(p, beta, beta_f, rhs, stacked, acc, acc_f, pay_a)
         push_pa = over(pay_a, sums_a, 4, False)
         start_all(push_pa, p.shards)
         sums_a[me] = pay_a[...]
@@ -772,8 +872,8 @@
         wait_all(push_pa, p.shards)
         total = total_of(sums_a, p.shards)
         made, energy = couple(p, total, pair)
-        build_coefs(p, made, coefs)
-        back_project(p, beta, coefs, res)
+        build_coefs(p, made, coefs, coefs_f)
+        back_project(p, beta, beta_f, coefs, coefs_f, res)
         wait_all(push_pb, p.shards)
         planes = total_of(sums_b, p.shards)
         norm0, alpha0 = [], []
@@ -792,7 +892,7 @@
         start_all(push_e, p.shards)
         held_e[me] = chunk_a[me]
         pay_stats(p, stats, pay_c)
-        project(p, beta, stacked, acc, pay_c)
+        project(p, beta, beta_f, res, stacked, acc, acc_f, pay_c)
         push_pc = over(pay_c, sums_c, 8, False)
         start_all(push_pc, p.shards)
         sums_c[me] = pay_c[...]
@@ -942,7 +1042,8 @@
         pltpu.VMEM((p.bands, p.grid, p.own), f32),
         pltpu.VMEM((p.bands, 8, LANES), f32),
         pltpu.VMEM((inters, LANES), f32),
-        pltpu.VMEM((p.shards, inters, LANES), f32),
+        pltpu.VMEM((8, inters), f32),
+        pltpu.VMEM((p.shards, 8, inters), f32),
         pltpu.VMEM((payload, LANES), f32),
         pltpu.VMEM(small, f32),
         pltpu.VMEM((few, LANES), f32),
@@ -952,10 +1053,13 @@
         pltpu.VMEM((few, LANES), f32),
         pltpu.VMEM(tiny, f32),
         pltpu.VMEM((SLOTS, 2, JB, p.grid, p.own), f32),
-        pltpu.VMEM((2, 2, p.count, p.grid, p.own), bf16),
+        pltpu.VMEM((2, 2, p.matrix, p.grid, p.own), bf16),
+        pltpu.VMEM((2, p.vector, p.grid, p.own), f32),
         pltpu.VMEM((p.grid // TALL, 4 * p.bands * TALL, p.own), bf16),
-        pltpu.VMEM((2, p.count, 8, 4 * p.bands * TALL), f32),
-        pltpu.VMEM((2, 2 * p.bands * TALL, 2 * p.count * TALL), bf16),
+        pltpu.VMEM((2, p.matrix, 8, 4 * p.bands * TALL), f32),
+        pltpu.VMEM((2 * p.bands, p.vector, 8, LANES), f32),
+        pltpu.VMEM((2, 2 * p.bands * TALL, 2 * p.matrix * TALL), bf16),
+        pltpu.VMEM((2 * p.bands, p.vector, LANES), f32),
         pltpu.VMEM((thick, p.grid, LANES), f32),
         pltpu.VMEM((dense_rows, LANES), f32),
         pltpu.VMEM((groups, dense_rows, LANES), jnp.int16 if coded else f32),
@@ -968,8 +1072,18 @@
         pltpu.SemaphoreType.DMA((10, p.shards - 1)),
         pltpu.SemaphoreType.DMA((3, groups - 1)),
         pltpu.SemaphoreType.DMA((3, groups - 1)),
-        pltpu.SemaphoreType.DMA((1,)),
+        pltpu.SemaphoreType.DMA((2,)),
+        pltpu.VMEM(mine, bf16),
+        pltpu.VMEM(dv.shape, f32),
+        pltpu.VMEM(vloc.shape, f32),
+        pltpu.VMEM(xy.shape, jnp.int32),
     ]
+    scratch += [
+        pltpu.VMEM(table.shape, bf16)
+        for table in (p.z_inv, p.z_fwd, p.y_inv, p.x_inv, p.x_fwd, p.y_fwd)
+    ]
+    scratch.append(pltpu.SemaphoreType.DMA((10,)))
+
     hbm = pl.BlockSpec(memory_space=pl.ANY)
     smem = pl.BlockSpec(memory_space=pltpu.SMEM)
     return pl.pallas_call(
@@ -977,7 +1091,7 @@
         out_shape=[
             spec_of(mine), spec_of((p.planes, wide_y * p.grid)),
         ],
-        in_specs=[VMEM] * 3 + [hbm, VMEM] + [smem] * 3 + [VMEM] * 6,
+        in_specs=[hbm] * 5 + [smem] * 3 + [hbm] * 6,
         out_specs=[hbm, VMEM],
         scratch_shapes=scratch,
         compiler_params=pltpu.CompilerParams(

time: 101 us -> 90 us (0.89)
  Pallas kernels: 100 us -> 89.2 us
    pallas_call x1, Pallas kernels: 98.6 us -> 87.3 us  [program(): pl.pallas_call(kernel, out_shape=[spec_of(mine), spec_of((p.planes, wide_...]
where the time goes in v3:
time: 90 us; the launch traced here: 89.8 us
  Pallas kernels  89.2 us (99%)
    pallas_call x1, Pallas kernels, program(): pl.pallas_call(kernel, out_shape=[spec_of(mine), spec_of((p.planes, wide_...  87.3 us
    pallas_call x1, Pallas kernels, settle(): pl.pallas_call(kernel, out_shape=[spec_of(x.shape) for x in arrays], in_s...  1.85 us

profile of v3, /device:TPU:0, one launch (start us, length us, event | category | flops | bytes accessed | tf_op | source)
XLA Modules:
  0.0 89.8 jit_solution(720780405185984143)
XLA Ops:
  0.6 87.3 %response.1 = (f32[2,2,96,256]{3,2,1,0:T(8,128)}, f32[12,2304]{1,0:T(8,128)}) custom-call(bf16[2,2,96,256]{3,2,1,0:T(8,128)(2,1)} %psi_h.1, f32[12,9216]{1,0:T(8,128)} %dv_h.1, f32[12,9216]{1,0:T(8,128)} %vloc_h.1, f32[2,128,96,256]{3,2,1,0:T(8,128)} %beta_hbm.1, s32[16,128]{1,0:T(8,128)} %bitcast.1, f32[2]{0:T(128)} %shift_r.1, f32[2,4,4]{2,1,0:T(4,128)} %dij_r.1, ...), custom_call_target="tpu_custom_call" | custom-call | tf_op jit(solution)/shard_map/response/pallas_call | solution.py:1089
  87.9 1.8 %settle.1 = (f32[2,2,96,256]{3,2,1,0:T(8,128)}, f32[12,2304]{1,0:T(8,128)}) custom-call(f32[2,2,96,256]{3,2,1,0:T(8,128)} %get-tuple-element.4.refs_0_, f32[12,2304]{1,0:T(8,128)} %get-tuple-element.5.refs_1_), custom_call_target="tpu_custom_call" | custom-call | tf_op jit(solution)/shard_map/settle/pallas_call | solution.py:728

commit v4 on v3

--- a/solution.py
+++ b/solution.py
@@ -195,7 +195,7 @@
             stat[b] = stat[b] + made[:, :LANES] + made[:, LANES:]
         return carry
 
-    lax.fori_loop(0, p.images, scaled, 0)
+    lax.fori_loop(0, p.images, scaled, 0, unroll=2)
     if spectrum is not None:
 
         def forth(b, carry):
@@ -906,6 +906,16 @@
         push_pd = over(pay_d, sums_d, 9, False)
         start_all(push_pd, p.shards)
         sums_d[me] = pay_d[...]
+
+        def products(at, carry):
+            to = aligned(at, p.grid)
+            one = field_p[to, :]
+            first, second = one * field_0[to, :], one * field_1[to, :]
+            spectrum[to, :LANES] = first[:, :LANES] + first[:, LANES:]
+            spectrum[to, LANES:] = second[:, :LANES] + second[:, LANES:]
+            return carry
+
+        lax.fori_loop(0, p.images, products, 0)
         wait_all(push_pc, p.shards)
         total = total_of(sums_c, p.shards)
         made, energy = couple(p, total, pair)
@@ -924,10 +934,8 @@
             made = 0.0
             for b in range(p.bands):
                 at = aligned(b * p.planes + zp, p.grid)
-                k2 = jnp.concatenate([keep[b], keep[b]], axis=1)
-                a2 = jnp.concatenate([alpha1[b], alpha1[b]], axis=1)
-                made = made + field_p[at, :] * (k2 * field_0[at, :] + a2 * field_1[at, :])
-            return 4.0 * (made[:, :LANES] + made[:, LANES:])
+                made = made + (keep[b] * spectrum[at, :LANES] + alpha1[b] * spectrum[at, LANES:])
+            return 4.0 * made
 
         lane = lax.broadcasted_iota(jnp.int32, (1, LANES), 1)
         if dense:

time: 90 us -> 89.6 us (level)
  no operation moved by 1% of the time
where the time goes in v4:
time: 89.6 us; the launch traced here: 89.4 us
  Pallas kernels  88.8 us (99%)
    pallas_call x1, Pallas kernels, program(): pl.pallas_call(kernel, out_shape=[spec_of(mine), spec_of((p.planes, wide_...  86.9 us
    pallas_call x1, Pallas kernels, settle(): pl.pallas_call(kernel, out_shape=[spec_of(x.shape) for x in arrays], in_s...  1.85 us

profile of v4, /device:TPU:0, one launch (start us, length us, event | category | flops | bytes accessed | tf_op | source)
XLA Modules:
  0.0 89.4 jit_solution(16623310166186106669)
XLA Ops:
  0.6 86.9 %response.1 = (f32[2,2,96,256]{3,2,1,0:T(8,128)}, f32[12,2304]{1,0:T(8,128)}) custom-call(bf16[2,2,96,256]{3,2,1,0:T(8,128)(2,1)} %psi_h.1, f32[12,9216]{1,0:T(8,128)} %dv_h.1, f32[12,9216]{1,0:T(8,128)} %vloc_h.1, f32[2,128,96,256]{3,2,1,0:T(8,128)} %beta_hbm.1, s32[16,128]{1,0:T(8,128)} %bitcast.1, f32[2]{0:T(128)} %shift_r.1, f32[2,4,4]{2,1,0:T(4,128)} %dij_r.1, ...), custom_call_target="tpu_custom_call" | custom-call | tf_op jit(solution)/shard_map/response/pallas_call | solution.py:1097
  87.5 1.8 %settle.1 = (f32[2,2,96,256]{3,2,1,0:T(8,128)}, f32[12,2304]{1,0:T(8,128)}) custom-call(f32[2,2,96,256]{3,2,1,0:T(8,128)} %get-tuple-element.4.refs_0_, f32[12,2304]{1,0:T(8,128)} %get-tuple-element.5.refs_1_), custom_call_target="tpu_custom_call" | custom-call | tf_op jit(solution)/shard_map/settle/pallas_call | solution.py:728
